TPU v7x, 32 devices: a 4x4x1 block of a 4x4x8 slice. The times are simulated.
32 devices in a mesh: dp: 1 (over z), tp: 32 (over y, x, core).
Axes of the slice: x: 4, y: 4, z: 1, core: 2. Of those that a mesh axis runs over, the one named last changes fastest.
The devices are a block of a 4x4x8 slice.
Arguments:
- hidden: bfloat16 [2048, 2048], P('dp')
- w_query: bfloat16 [2048, 2048], P(None, 'tp')
- w_key: bfloat16 [2048, 128], replicated
- w_value: bfloat16 [2048, 128], replicated
- w_out: bfloat16 [2048, 2048], P('tp')
- k_cache: bfloat16 [2048, 256, 128], P(('dp', 'tp'))
- v_cache: bfloat16 [2048, 256, 128], P(('dp', 'tp'))
- lengths: int32 [2048], P('dp')
Outputs:
- output 1: bfloat16 [2048, 2048], P('dp', 'tp')
- output 2: bfloat16 [2048, 256, 128], P(('dp', 'tp'))
- output 3: bfloat16 [2048, 256, 128], P(('dp', 'tp'))
All inputs are finite; a program needn't handle non-finite values.
Results may differ from a plain program's by a relative error of at most 0.0145829.
Values are sent between devices in bfloat16 or wider.
A program may use at most 768 MiB of HBM per device.

v0:
```python
import jax
import jax.numpy as jnp
from jax import lax
from jax.sharding import PartitionSpec as P


def rope_angles(positions, head_dim):
    half_dim = head_dim // 2
    inv_freq = 10000.0 ** (-(jnp.arange(half_dim, dtype=jnp.float32) * 2.0) / head_dim)
    return positions.astype(jnp.float32)[:, None] * inv_freq[None, :]


def apply_rope(values_in, angles):
    half_dim = values_in.shape[-1] // 2
    first_half = values_in[..., :half_dim]
    second_half = values_in[..., half_dim:]
    cosines = jnp.cos(angles)
    sines = jnp.sin(angles)
    return jnp.concatenate([first_half * cosines - second_half * sines, second_half * cosines + first_half * sines], axis=-1)


def attend(q_rot, k_all, v_all, lengths):
    head_dim = q_rot.shape[-1]
    seq_len = k_all.shape[1]
    scores = jnp.einsum('bhd,bsd->bhs', q_rot, k_all, preferred_element_type=jnp.float32) * (head_dim ** -0.5)
    valid_mask = lax.broadcasted_iota(jnp.int32, (1, 1, seq_len), 2) <= lengths[:, None, None]
    scores = jnp.where(valid_mask, scores, -1e30)
    row_max = jnp.max(scores, axis=-1, keepdims=True)
    weights = jnp.exp(scores - row_max)
    denominator = jnp.sum(weights, axis=-1, keepdims=True)
    summed = jnp.einsum('bhs,bsd->bhd', weights.astype(jnp.bfloat16), v_all, preferred_element_type=jnp.float32)
    return (summed / denominator).astype(jnp.bfloat16)


def solution(mesh):
    group_size = mesh.shape['tp']
    cache_spec = P(('dp', 'tp'), None, None)

    def local_step(hidden, w_query, w_key, w_value, w_out, k_cache, v_cache, lengths):
        rows_dev, seq_len, head_dim = k_cache.shape
        cols_dev = w_query.shape[1]
        num_heads = cols_dev * group_size // head_dim
        row_start = lax.axis_index('tp') * rows_dev
        q_cols = jnp.dot(hidden, w_query, preferred_element_type=jnp.float32).astype(jnp.bfloat16)
        q_rows = lax.all_to_all(q_cols, 'tp', 0, 1, tiled=True)
        own_hidden = lax.dynamic_slice_in_dim(hidden, row_start, rows_dev, axis=0)
        own_lengths = lax.dynamic_slice_in_dim(lengths, row_start, rows_dev, axis=0)
        k_new = jnp.dot(own_hidden, w_key, preferred_element_type=jnp.float32).astype(jnp.bfloat16)
        v_new = jnp.dot(own_hidden, w_value, preferred_element_type=jnp.float32).astype(jnp.bfloat16)
        angles = rope_angles(own_lengths, head_dim)
        q_heads = q_rows.reshape(rows_dev, num_heads, head_dim).astype(jnp.float32)
        q_rot = apply_rope(q_heads, angles[:, None, :]).astype(jnp.bfloat16)
        k_rot = apply_rope(k_new.astype(jnp.float32), angles).astype(jnp.bfloat16)
        new_slot = (lax.broadcasted_iota(jnp.int32, (1, seq_len), 1) == own_lengths[:, None])[:, :, None]
        k_out = jnp.where(new_slot, k_rot[:, None, :], k_cache)
        v_out = jnp.where(new_slot, v_new[:, None, :], v_cache)
        attn_out = attend(q_rot, k_out, v_out, own_lengths)
        o_cols = lax.all_to_all(attn_out.reshape(rows_dev, num_heads * head_dim), 'tp', 1, 0, tiled=True)
        y_part = jnp.dot(o_cols, w_out, preferred_element_type=jnp.float32).astype(jnp.bfloat16)
        y_local = lax.psum_scatter(y_part, 'tp', scatter_dimension=1, tiled=True)
        return y_local, k_out, v_out

    return jax.shard_map(
        local_step,
        mesh=mesh,
        in_specs=(P('dp', None), P(None, 'tp'), P(), P(), P('tp', None), cache_spec, cache_spec, P('dp')),
        out_specs=(P('dp', 'tp'), cache_spec, cache_spec),
        check_vma=False,
    )
```

profile of v0, /device:TPU:97, one launch (start us, length us, event | category | flops | bytes accessed | tf_op | source)
XLA Modules:
  0.0 154.0 jit_solution(2921614557427456188)
XLA Ops:
  7.2 0.0 copy-start
  7.2 6.1 %convolution_convert_fusion.1 = bf16[2048,64]{0,1:T(8,128)(2,1)S(1)} fusion(bf16[2048,2048]{1,0:T(8,128)(2,1)} %param.8, bf16[2048,64]{0,1:T(8,128)(2,1)} %param.9), kind=kOutput, calls=%fused_computation.3 | convolution fusion | flops 537001984 | bytes 8912896 | tf_op jit(solution)/shard_map/dot_general | solution.py:44
  13.3 0.5 all_to_all.24
  13.8 0.2 copy.23
  14.0 1.1 reshape.133
  15.1 9.1 %all-to-all-start = ((bf16[32,2,2048]{2,1,0:T(2,128)(2,1)}), bf16[32,2,2048]{2,1,0:T(2,128)(2,1)S(1)}, u32[]{:S(2)}, u32[]{:S(2)}) async-start(bf16[32,2,2048]{2,1,0:T(2,128)(2,1)} %reshape.133), calls=%async_computation | async-start | bytes 524288 | tf_op jit(solution)/shard_map/all_to_all | solution.py:45
  24.3 0.1 reduce-scatter.2.cloned.1.call-start
  24.4 0.8 fusion.15
  25.1 1.2 convolution_convert_fusion.2
  26.3 1.2 fusion.2
  27.5 0.1 iota_compare_fusion.1
  27.6 0.2 multiply_cosine_fusion
  27.8 0.1 pad_maximum_fusion
  27.9 9.8 %broadcast_select_fusion.1 = (bf16[64,256,128]{2,1,0:T(8,128)(2,1)}, bf16[64,256,128]{2,1,0:T(8,128)(2,1)}) fusion(bf16[64,256,128]{2,1,0:T(8,128)(2,1)} %param.13, pred[64,256]{1,0:T(8,128)(4,1)S(1)} %get-tuple-element.18, bf16[64,128]{1,0:T(8,128)(2,1)S(1)} %pad_maximum_fusion, bf16[64,256,128]{2,1,0:T(8,128)(2,1)} %param.14, ...), kind=kLoop, calls=%fused_computation.2 | loop fusion | flops 4194304 | bytes 16826368 | tf_op jit(solution)/shard_map/jit(_where)/select_n | solution.py:55
  37.7 0.4 reshape.134
  38.0 0.1 bitcast_convert_fusion
  38.2 0.1 fusion.16
  38.2 0.3 copy.21
  38.5 0.3 copy.20
  38.8 0.1 subtract_convert_fusion
  39.0 3.7 %fusion.17 = (f32[64,16]{1,0:T(8,128)S(1)}, f32[64,16,256]{2,1,0:T(8,128)S(1)}) fusion(bf16[64,256,128]{2,1,0:T(8,128)(2,1)} %get-tuple-element.11, bf16[64,16,64]{2,1,0:T(8,128)(2,1)S(1)} %get-tuple-element.6, bf16[64,16,64]{2,1,0:T(8,128)(2,1)S(1)} %get-tuple-element.5, pred[64,256]{1,0:T(8,128)(4,1)S(1)} %get-tuple-element.17), kind=kOutput, calls=%fused_computation.35 | convolution fusion | flops 68418560 | bytes 5525504 | tf_op jit(solution)/shard_map/bhd,bsd->bhs/dot_general | solution.py:25
  42.6 0.4 fusion.3
  43.0 0.8 fusion.1
  43.8 0.3 copy.19
  44.1 0.4 reshape.135
  44.5 14.9 %all_to_all.32 = bf16[32,2,2048]{2,1,0:T(2,128)(2,1)S(1)} all-to-all(bf16[32,2,2048]{2,1,0:T(2,128)(2,1)S(1)} %reshape.135), channel_id=1, replica_groups=mesh['dp'=1,'tp'=32] {'tp'}, dimensions={0} | all-to-all | bytes 524288 | tf_op jit(solution)/shard_map/all_to_all | solution.py:58
  59.4 0.4 reshape.136
  59.8 0.3 copy.17
  60.1 0.5 all_to_all.29
  60.6 5.6 %convolution_convert_fusion = bf16[2048,2048]{0,1:T(8,128)(2,1)} fusion(bf16[2048,64]{0,1:T(8,128)(2,1)S(1)} %all_to_all.29, bf16[64,2048]{1,0:T(8,128)(2,1)S(1)} %copy-done.3), kind=kOutput, calls=%fused_computation | convolution fusion | flops 541065216 | bytes 8912896 | tf_op jit(solution)/shard_map/dot_general | solution.py:59
  66.2 0.1 reduce-scatter.2.cloned.1.call-update
  66.3 80.9 %reduce-scatter.2.cloned.1.call-done = bf16[2048,64]{0,1:T(8,128)(2,1)} async-done(((bf16[2048,2048]{0,1:T(8,128)(2,1)}), bf16[2048,64]{0,1:T(8,128)(2,1)}) %reduce-scatter.2.cloned.1.call-update) | async-done | bytes 262160 | tf_op jit(solution)/shard_map/reduce_scatter | solution.py:60
  (10 shorter events, 0.1 us)
Async XLA Ops:
  7.2 18.0 %copy-start = (bf16[2048,128]{1,0:T(8,128)(2,1)S(1)}, bf16[2048,128]{1,0:T(8,128)(2,1)}, u32[]{:S(2)}) copy-start(bf16[2048,128]{1,0:T(8,128)(2,1)} %param.11) | copy-start | bytes 1572868
  13.3 13.0 %copy-start.2 = (bf16[2048,128]{1,0:T(8,128)(2,1)S(1)}, bf16[2048,128]{1,0:T(8,128)(2,1)}, u32[]{:S(2)}) copy-start(bf16[2048,128]{1,0:T(8,128)(2,1)} %param.10) | copy-start | bytes 1572868
  15.1 22.5 %all-to-all-start = ((bf16[32,2,2048]{2,1,0:T(2,128)(2,1)}), bf16[32,2,2048]{2,1,0:T(2,128)(2,1)S(1)}, u32[]{:S(2)}, u32[]{:S(2)}) async-start(bf16[32,2,2048]{2,1,0:T(2,128)(2,1)} %reshape.133), calls=%async_computation | async-start | bytes 524288 | tf_op jit(solution)/shard_map/all_to_all | solution.py:45
  24.3 122.9 %reduce-scatter.2.cloned.1.call-start = ((), (), s32[]{:S(2)}) async-start(), calls=%async_computation.3 | async-start | bytes 8650752 | tf_op jit(solution)/shard_map/reduce_scatter | solution.py:60
  38.8 4.2 %copy-start.1 = (bf16[64,256,128]{2,1,0:T(8,128)(2,1)S(1)}, bf16[64,256,128]{2,1,0:T(8,128)(2,1)}, u32[]{:S(2)}) copy-start(bf16[64,256,128]{2,1,0:T(8,128)(2,1)} %get-tuple-element.12) | copy-start | bytes 12582916
  43.8 16.8 %copy-start.3 = (bf16[64,2048]{1,0:T(8,128)(2,1)S(1)}, bf16[64,2048]{1,0:T(8,128)(2,1)}, u32[]{:S(2)}) copy-start(bf16[64,2048]{1,0:T(8,128)(2,1)} %param.12) | copy-start | bytes 786436
Sparse Core Ops, SparseCore 0:
  66.4 80.7 reduce-scatter.1
where the time goes:
time: 155 us; the launch traced here: 154 us
  waiting for transfers between devices  81 us (52%)
  matrix products  18.5 us (12%)
  blocking collectives  14.9 us (10%)
  between operations  14.3 us (9%)
  other arithmetic  11.6 us (7%)
  starting transfers between devices  9.2 us (6%)
  local copies, waits for them, and re-layouts  4.73 us (3%)
    reduce_scatter x1, waiting for transfers between devices, local_step(): y_local = lax.psum_scatter(y_part, 'tp', scatter_dimension=1, tiled=True)  80.9 us
    all_to_all x1, blocking collectives, local_step(): lax.all_to_all(attn_out.reshape(rows_dev, num_heads * head_dim), 'tp', 1,...  14.9 us
    select_n x1, other arithmetic, local_step(): k_out = jnp.where(new_slot, k_rot[:, None, :], k_cache)  9.79 us
    all_to_all x1, starting transfers between devices, local_step(): q_rows = lax.all_to_all(q_cols, 'tp', 0, 1, tiled=True)  9.14 us
    dot_general x1, matrix products, local_step(): jnp.dot(hidden, w_query, preferred_element_type=jnp.float32)  6.09 us
    dot_general x1, matrix products, local_step(): jnp.dot(o_cols, w_out, preferred_element_type=jnp.float32)  5.62 us
    dot_general x1, matrix products, attend(): jnp.einsum('bhd,bsd->bhs', q_rot, k_all, preferred_element_type=jnp.float32)  3.66 us
  transfers between devices with their start and end apart: 2, of which 1 were waited for; matrix products, arithmetic and copies ran while one was open for 9% of the time, Pallas kernels for 0%

commit v1 on v0

v1 whole, which is shorter than its diff:
```python
import functools
import math

import jax
import jax.numpy as jnp
from jax import lax
from jax.experimental import pallas as pl
from jax.experimental.pallas import tpu as pltpu
from jax.sharding import PartitionSpec as P

F32, BF16 = jnp.float32, jnp.bfloat16
MESH = pl.DeviceIdType.MESH
TILE = 16
CACHE_STEPS = 8
O_STEPS = 4


def rope_tables(positions, head_dim):
    half_dim = head_dim // 2
    inv_freq = 10000.0 ** (-(jnp.arange(half_dim, dtype=F32) * 2.0) / head_dim)
    angles = positions.astype(F32)[:, None] * inv_freq[None, :]
    return jnp.cos(angles), jnp.sin(angles)


def cache_kernel(lens, hidden, w_key, w_value, cos, sin, k_in, v_in, k_out, v_out,
                 k_buf, v_buf, h_buf, wk_buf, wv_buf, k_new, v_new, in_sem, out_sem, small_sem):
    rows, seq, dim = k_in.shape
    step_rows = rows // CACHE_STEPS
    first = lax.axis_index("tp") * rows
    small = [
        pltpu.make_async_copy(hidden.at[pl.ds(first, rows)], h_buf, small_sem.at[0]),
        pltpu.make_async_copy(w_key, wk_buf, small_sem.at[1]),
        pltpu.make_async_copy(w_value, wv_buf, small_sem.at[2]),
    ]
    for copy in small:
        copy.start()
    pairs = ((k_in, k_buf, k_out), (v_in, v_buf, v_out))
    ins, outs = [], []
    for j in range(CACHE_STEPS):
        part = pl.ds(j * step_rows, step_rows)
        ins.append([pltpu.make_async_copy(src.at[part], buf.at[part], in_sem.at[i, j]) for i, (src, buf, _) in enumerate(pairs)])
        outs.append([pltpu.make_async_copy(buf.at[part], dst.at[part], out_sem.at[i, j]) for i, (_, buf, dst) in enumerate(pairs)])
        for copy in ins[j]:
            copy.start()
    for copy in small:
        copy.wait()
    half = dim // 2
    key = jnp.dot(h_buf[...], wk_buf[...], preferred_element_type=F32).astype(BF16).astype(F32)
    x1, x2, c, s = key[:, :half], key[:, half:], cos[...], sin[...]
    k_new[...] = jnp.concatenate([x1 * c - x2 * s, x2 * c + x1 * s], axis=1)
    v_new[...] = jnp.dot(h_buf[...], wv_buf[...], preferred_element_type=F32)
    slot = lax.broadcasted_iota(jnp.int32, (TILE, dim), 0)
    for j in range(CACHE_STEPS):
        for copy in ins[j]:
            copy.wait()
        for r in range(j * step_rows, (j + 1) * step_rows):
            position = lens[r]
            start = pl.multiple_of((position // TILE) * TILE, TILE)
            here = slot == position - start
            for buf, new in ((k_buf, k_new), (v_buf, v_new)):
                old = buf[r, pl.ds(start, TILE), :].astype(F32)
                buf[r, pl.ds(start, TILE), :] = jnp.where(here, new[pl.ds(r, 1), :], old).astype(BF16)
        for copy in outs[j]:
            copy.start()
    for step in outs:
        for copy in step:
            copy.wait()


def step_kernel(side, hidden, w_query, w_out, k_all, v_all, lens, cos, sin, y_out,
                h_buf, wq_buf, wo_buf, w_buf, k_buf, v_buf, q_send, q_recv, q_rows, o_rows, o_buf,
                y_send, y_recv,
                h_sem, wq_sem, wo_sem, k_sem, v_sem, q_ssem, q_rsem, w_ssem, w_rsem, o_ssem, o_rsem, y_ssem, y_rsem):
    rows, seq, dim = k_all.shape
    half = dim // 2
    pack = rows // 2
    group = 2 * side * side
    heads = group // 2
    cols = w_buf.shape[1]
    me = lax.axis_index("tp")
    core = lax.rem(me, 2)
    chip = me // 2
    x = lax.rem(chip, side)
    y = chip // side

    def index(xx, yy, cc):
        return (lax.rem(yy, side) * side + lax.rem(xx, side)) * 2 + cc

    def remote(src, dst, ssem, rsem, target):
        return pltpu.make_async_remote_copy(src_ref=src, dst_ref=dst, send_sem=ssem, recv_sem=rsem,
                                            device_id={"tp": target}, device_id_type=MESH)

    block = rows * 2 * side
    ydest = [lax.rem(y + d, side) for d in (2, 1, 3, 0)]

    def h_part(yy):
        return pl.ds(pl.multiple_of(yy * block, block), block)

    wq_copy = pltpu.make_async_copy(w_query, wq_buf, wq_sem)
    wq_copy.start()
    h_copies = [pltpu.make_async_copy(hidden.at[h_part(yy)], h_buf.at[h_part(yy)], h_sem.at[i]) for i, yy in enumerate(ydest)]
    for copy in h_copies:
        copy.start()
    wo_copies = []
    for i in range(side):
        wo_copies.append(pltpu.make_async_copy(w_out.at[:, pl.ds(i * cols, cols)], wo_buf.at[i], wo_sem.at[i]))
        wo_copies[i].start()
    step_rows = rows // O_STEPS
    kv_copies = []
    for k in range(O_STEPS):
        part = pl.ds(k * step_rows, step_rows)
        kv_copies.append((pltpu.make_async_copy(k_all.at[part], k_buf.at[part], k_sem.at[k]),
                          pltpu.make_async_copy(v_all.at[part], v_buf.at[part], v_sem.at[k])))
        for copy in kv_copies[k]:
            copy.start()

    barrier = pltpu.get_barrier_semaphore()
    peers = [(lax.rem(chip + i, heads)) * 2 + c for i in range(1, heads) for c in range(2)] + [chip * 2 + (1 - core)]
    for peer in peers:
        pl.semaphore_signal(barrier, inc=1, device_id={"tp": peer}, device_id_type=MESH)

    wq_copy.wait()
    sends = []
    for i, yy in enumerate(ydest):
        h_copies[i].wait()
        q_val = jnp.dot(h_buf[h_part(yy), :], wq_buf[...], preferred_element_type=F32).astype(BF16)
        q_val = q_val.reshape(2 * side, 2, pack, half)
        q_send[i] = jnp.concatenate([q_val[:, 0], q_val[:, 1]], axis=-1)
        if i == 0:
            pl.semaphore_wait(barrier, len(peers))

        def send_q(j, carry, i=i, yy=yy):
            slot = lax.rem(j + x * 2 + 2, 2 * side)
            target = yy * 2 * side + slot
            remote(q_send.at[i, slot], q_recv.at[me], q_ssem.at[i * 2 * side + slot], q_rsem.at[me], target).start()
            return carry

        if i < side - 1:
            lax.fori_loop(0, 2 * side, send_q, 0)
        else:
            own = x * 2 + core

            def send_own_row(j, carry, i=i, yy=yy):
                slot = lax.rem(own + 1 + j, 2 * side)
                target = yy * 2 * side + slot
                remote(q_send.at[i, slot], q_recv.at[me], q_ssem.at[i * 2 * side + slot], q_rsem.at[me], target).start()
                return carry

            lax.fori_loop(0, 2 * side - 1, send_own_row, 0)
            q_recv[me] = q_send[i, own]

    def w_slot(t):
        return w_buf.at[pl.ds(pl.multiple_of(t * half, half), half)]

    for copy in wo_copies:
        copy.wait()
    n_w = [0]

    def send_w(src, t, target):
        copy = remote(src, w_slot(t), w_ssem.at[n_w[0]], w_rsem.at[t], target)
        n_w[0] += 1
        copy.start()
        sends.append(copy)

    def wait_w(t):
        remote(w_slot(t), w_slot(t), w_ssem.at[0], w_rsem.at[t], me).wait_recv()

    w_buf[pl.ds(pl.multiple_of(me * half, half), half)] = wo_buf[y]
    for d in (1, 3, 2):
        send_w(wo_buf.at[lax.rem(y + d, side)], me, index(x, y + d, core))
    left, right, other = index(x + side - 1, y, core), index(x + 1, y, core), chip * 2 + (1 - core)
    for target in (right, left, other):
        send_w(wo_buf.at[y], me, target)

    def forward_column(d):
        t = index(x, y + d, core)
        wait_w(t)
        for target in (right, left, other):
            send_w(w_slot(t), t, target)

    for d in (1, 3, 2):
        forward_column(d)

    lane = lax.broadcasted_iota(jnp.int32, (pack, dim), 1) < half
    c_low, c_high = cos[pl.ds(0, pack), :], cos[pl.ds(pack, pack), :]
    s_low, s_high = sin[pl.ds(0, pack), :], sin[pl.ds(pack, pack), :]
    c_pack = jnp.concatenate([c_low, c_high], axis=1)
    s_pack = jnp.concatenate([s_low, s_high], axis=1)
    for i in range(1, group):
        t = lax.rem(me + i, group)
        remote(q_recv.at[t], q_recv.at[t], q_ssem.at[0], q_rsem.at[t], me).wait_recv()
    for i in range(heads):
        p1, p2 = q_recv[2 * i].astype(F32), q_recv[2 * i + 1].astype(F32)
        r1, r2 = p1 * c_pack - p2 * s_pack, p2 * c_pack + p1 * s_pack
        q_rows[pl.ds(i, pack, stride=heads), :] = jnp.where(lane, r1, pltpu.roll(r2, half, 1))
        q_rows[pl.ds(pack * heads + i, pack, stride=heads), :] = jnp.where(lane, pltpu.roll(r1, half, 1), r2)

    def relay_right(d):
        t = index(x + side - 1, y + d, core)
        wait_w(t)
        send_w(w_slot(t), t, right)
        send_w(w_slot(t), t, other)

    def relay_left(d):
        t = index(x + 1, y + d, core)
        wait_w(t)
        send_w(w_slot(t), t, left)
        send_w(w_slot(t), t, other)

    def pass_on(xx, d):
        t = index(xx, y + d, core)
        wait_w(t)
        send_w(w_slot(t), t, other)

    scale = dim ** -0.5
    slots = lax.broadcasted_iota(jnp.int32, (heads, seq), 1)
    up, down = index(x, y + 1, core), index(x, y + side - 1, core)
    y_up, y_down, y_far = lax.rem(y + 1, side), lax.rem(y + side - 1, side), lax.rem(y + 2, side)
    n_o = [0]

    def send_o(yy, k, target):
        copy = remote(o_buf.at[yy, k], o_buf.at[yy, k], o_ssem.at[n_o[0]], o_rsem.at[yy, k], target)
        n_o[0] += 1
        copy.start()
        sends.append(copy)

    def wait_o(yy, k):
        remote(o_buf.at[yy, k], o_buf.at[yy, k], o_ssem.at[0], o_rsem.at[yy, k], me).wait_recv()

    def relay_o(k):
        if k % 2 == 0:
            wait_o(y_down, k)
            send_o(y_down, k, up)
        else:
            wait_o(y_up, k)
            send_o(y_up, k, down)

    def attend(k):
        for copy in kv_copies[k]:
            copy.wait()

        def some_rows(j, carry):
            for u in range(8):
                part = j * 8 + u
                r = k * step_rows + part
                q_row = q_rows[pl.ds(pl.multiple_of(r * heads, heads), heads), :].astype(BF16)
                scores = lax.dot_general(q_row, k_buf[r], (((1,), (1,)), ((), ())), preferred_element_type=F32) * scale
                scores = jnp.where(slots <= lens[pl.ds(r, 1), :], scores, -1e30)
                weights = jnp.exp(scores - jnp.max(scores, axis=1, keepdims=True))
                total = jnp.sum(weights, axis=1, keepdims=True)
                summed = jnp.dot(weights.astype(BF16), v_buf[r], preferred_element_type=F32)
                o_rows[pl.ds(pl.multiple_of(part * heads, heads), heads), :] = summed / total
            return carry

        lax.fori_loop(0, step_rows // 8, some_rows, 0)
        for i in range(heads):
            o_buf[y, k, i] = o_rows[pl.ds(i, step_rows, stride=heads), :].astype(BF16)
        send_o(y, k, up)
        send_o(y, k, down)

    attend(0)
    relay_right(0)
    relay_left(3)
    attend(1)
    relay_right(1)
    relay_left(2)
    pass_on(x + side - 1, 2)
    pass_on(x + side - 1, 3)
    attend(2)
    relay_o(0)
    pass_on(x + 1, 0)
    pass_on(x + 1, 1)
    attend(3)
    relay_o(1)
    for d in (0, 3, 1, 2):
        pass_on(x + 2, d)
    for i in range(heads):
        wait_w(2 * i + 1 - core)

    y_sends = []

    def project(yy):
        lhs = jnp.concatenate([o_buf[yy, :, i].reshape(rows, dim) for i in range(heads)], axis=1)
        res = jnp.dot(lhs, w_buf[...], preferred_element_type=F32).astype(BF16)
        row_owner = index(x, yy, core)
        n = len(y_sends)
        y_sends.append(yy)
        for slot in range(2 * side):
            part = res[:, slot * half:(slot + 1) * half]
            y_send[n, slot] = jnp.concatenate([part[:pack], part[pack:]], axis=1)
        own = x * 2 + core

        def send_y(j, carry):
            slot = lax.rem(own + 1 + j, 2 * side)
            target = y * 2 * side + slot
            remote(y_send.at[n, slot], y_recv.at[row_owner], y_ssem.at[n * 2 * side + slot], y_rsem.at[row_owner], target).start()
            return carry

        lax.fori_loop(0, 2 * side - 1, send_y, 0)
        y_recv[row_owner] = y_send[n, own]

    project(y)
    relay_o(2)
    relay_o(3)
    wait_o(y_up, 0)
    wait_o(y_up, 2)
    project(y_up)
    wait_o(y_down, 1)
    wait_o(y_down, 3)
    project(y_down)
    for k in range(O_STEPS):
        wait_o(y_far, k)
    project(y_far)

    own = x * 2 + core
    for yy in (y, y_up, y_down, y_far):
        def wait_y(j, carry, yy=yy):
            slot = lax.rem(own + 1 + j, 2 * side)
            t = yy * 2 * side + slot
            remote(y_recv.at[t], y_recv.at[t], y_ssem.at[0], y_rsem.at[t], me).wait_recv()
            return carry

        lax.fori_loop(0, 2 * side - 1, wait_y, 0)
    y_out[...] = y_recv[...]

    for copy in sends:
        copy.wait_send()

    def drain_q(j, carry):
        i, slot = j // (2 * side), lax.rem(j, 2 * side)
        remote(q_send.at[i, slot], q_recv.at[me], q_ssem.at[j], q_rsem.at[me], me).wait_send()
        return carry

    lax.fori_loop(0, (side - 1) * 2 * side, drain_q, 0)

    def drain_own(j, carry):
        slot = lax.rem(own + 1 + j, 2 * side)
        i = side - 1
        remote(q_send.at[i, slot], q_recv.at[me], q_ssem.at[i * 2 * side + slot], q_rsem.at[me], me).wait_send()
        for n in range(side):
            remote(y_send.at[n, slot], y_recv.at[me], y_ssem.at[n * 2 * side + slot], y_rsem.at[me], me).wait_send()
        return carry

    lax.fori_loop(0, 2 * side - 1, drain_own, 0)


def solution(mesh):
    group = mesh.shape["tp"]
    side = math.isqrt(group // 2)
    cache_spec = P(("dp", "tp"), None, None)
    vmem, hbm = pl.BlockSpec(memory_space=pltpu.VMEM), pl.BlockSpec(memory_space=pl.ANY)
    smem = pl.BlockSpec(memory_space=pltpu.SMEM)
    dma = pltpu.SemaphoreType.DMA

    def local_step(hidden, w_query, w_key, w_value, w_out, k_cache, v_cache, lengths):
        rows, seq, dim = k_cache.shape
        batch, embed = hidden.shape
        half = dim // 2
        heads = group * w_query.shape[1] // dim
        cols = w_out.shape[1] // side
        own_lengths = lax.dynamic_slice_in_dim(lengths, lax.axis_index("tp") * rows, rows, axis=0)
        cos, sin = rope_tables(own_lengths, dim)
        lens = jnp.broadcast_to(own_lengths[:, None], (rows, seq))
        cache_shape = jax.ShapeDtypeStruct(k_cache.shape, k_cache.dtype)
        k_out, v_out = pl.pallas_call(
            cache_kernel,
            out_shape=(cache_shape, cache_shape),
            in_specs=[smem, hbm, hbm, hbm, vmem, vmem, hbm, hbm],
            out_specs=(hbm, hbm),
            scratch_shapes=[
                pltpu.VMEM((rows, seq, dim), BF16), pltpu.VMEM((rows, seq, dim), BF16),
                pltpu.VMEM((rows, embed), BF16), pltpu.VMEM((embed, dim), BF16), pltpu.VMEM((embed, dim), BF16),
                pltpu.VMEM((rows, dim), F32), pltpu.VMEM((rows, dim), F32),
                dma((2, CACHE_STEPS)), dma((2, CACHE_STEPS)), dma((3,)),
            ],
            compiler_params=pltpu.CompilerParams(vmem_limit_bytes=24 << 20),
            name="cache_update",
        )(own_lengths, hidden, w_key, w_value, cos, sin, k_cache, v_cache)
        y_packed = pl.pallas_call(
            functools.partial(step_kernel, side),
            out_shape=jax.ShapeDtypeStruct((group, rows // 2, dim), BF16),
            in_specs=[hbm] * 5 + [vmem] * 3,
            out_specs=vmem,
            scratch_shapes=[
                pltpu.VMEM((batch, embed), BF16), pltpu.VMEM(w_query.shape, BF16),
                pltpu.VMEM((side, half, cols), BF16), pltpu.VMEM((group * half, cols), BF16),
                pltpu.VMEM((rows, seq, dim), BF16), pltpu.VMEM((rows, seq, dim), BF16),
                pltpu.VMEM((side, 2 * side, rows // 2, dim), BF16), pltpu.VMEM((group, rows // 2, dim), BF16),
                pltpu.VMEM((rows * heads, dim), F32), pltpu.VMEM((rows // O_STEPS * heads, dim), F32),
                pltpu.VMEM((side, O_STEPS, heads, rows // O_STEPS, dim), BF16),
                pltpu.VMEM((side, 2 * side, rows // 2, dim), BF16), pltpu.VMEM((group, rows // 2, dim), BF16),
                dma((side,)), dma, dma((side,)), dma((O_STEPS,)), dma((O_STEPS,)),
                dma((group,)), dma((group,)), dma((2 * group,)), dma((group,)),
                dma((4 * O_STEPS,)), dma((side, O_STEPS)), dma((group,)), dma((group,)),
            ],
            compiler_params=pltpu.CompilerParams(collective_id=0, has_side_effects=True, vmem_limit_bytes=48 << 20),
            name="attention_step",
        )(hidden, w_query, w_out, k_out, v_out, lens, cos, sin)
        y_local = y_packed.reshape(group, rows // 2, 2, half).transpose(0, 2, 1, 3).reshape(batch, half)
        return y_local, k_out, v_out

    return jax.shard_map(
        local_step,
        mesh=mesh,
        in_specs=(P("dp", None), P(None, "tp"), P(), P(), P("tp", None), cache_spec, cache_spec, P("dp")),
        out_specs=(P("dp", "tp"), cache_spec, cache_spec),
        check_vma=False,
    )
```

time: 155 us -> 70.9 us (0.46)
  waiting for transfers between devices: 81 us -> 0 us
  Pallas kernels: 0 us -> 54.3 us
  matrix products: 18.5 us -> 0 us
  blocking collectives: 14.9 us -> 0 us
  between operations: 14.3 us -> 0.71 us
  other arithmetic: 11.6 us -> 0.97 us
  local copies, waits for them, and re-layouts: 4.73 us -> 14.6 us
  starting transfers between devices: 9.2 us -> 0 us
    reduce_scatter x1 -> x0, waiting for transfers between devices: 80.9 us -> none  [local_step(): y_local = lax.psum_scatter(y_part, 'tp', scatter_dimension=1, tiled=True)]
    pallas_call x0 -> x2, Pallas kernels: none -> 54.3 us  [the longest x1 49.1 us: local_step(): pl.pallas_call(functools.partial(step_kernel, side), out_shape=jax.ShapeD...]
    dot_general x6 -> x0, matrix products: 18.5 us -> none  [the longest x1 6.09 us: local_step(): jnp.dot(hidden, w_query, preferred_element_type=jnp.float32)]
    all_to_all x1 -> x0, blocking collectives: 14.9 us -> none  [local_step(): lax.all_to_all(attn_out.reshape(rows_dev, num_heads * head_dim), 'tp', 1,...]
    unnamed x14 -> x16, local copies, waits for them, and re-layouts: 2.78 us -> 14.2 us
    select_n x1 -> x0, other arithmetic: 9.79 us -> none  [local_step(): k_out = jnp.where(new_slot, k_rot[:, None, :], k_cache)]
    all_to_all x1 -> x0, starting transfers between devices: 9.14 us -> none  [local_step(): q_rows = lax.all_to_all(q_cols, 'tp', 0, 1, tiled=True)]
    all_to_all x6 -> x0, local copies, waits for them, and re-layouts: 1.88 us -> none  [the longest x4 1.17 us: local_step(): lax.all_to_all(attn_out.reshape(rows_dev, num_heads * head_dim), 'tp', 1,...]
  transfers between devices with their start and end apart: 2 -> 0, of which waited for: 1 -> 0; matrix products, arithmetic and copies ran while one was open for 9% -> 0% of each run, Pallas kernels for 0% -> 0%
where the time goes in v1:
time: 70.9 us; the launch traced here: 70.5 us
  Pallas kernels  54.3 us (77%)
  local copies, waits for them, and re-layouts  14.6 us (21%)
  other arithmetic  0.97 us (1%)
  between operations  0.71 us (1%)
    pallas_call x1, Pallas kernels, local_step(): pl.pallas_call(functools.partial(step_kernel, side), out_shape=jax.ShapeD...  49.1 us
    unnamed x16, local copies, waits for them, and re-layouts  14.2 us
    pallas_call x1, Pallas kernels, local_step(): pl.pallas_call(cache_kernel, out_shape=(cache_shape, cache_shape), in_spe...  5.16 us

profile of v1, /device:TPU:97, one launch (start us, length us, event | category | flops | bytes accessed | tf_op | source)
XLA Modules:
  0.0 70.5 jit_solution(6555132127113090440)
XLA Ops:
  0.6 0.8 %fusion = (f32[64]{0:T(128)S(1)}, s32[64]{0:T(128)S(1)}) fusion(s32[2048]{0:T(1024)} %param.15, s32[]{:T(128)S(6)} %select_n.3), kind=kLoop, calls=%fused_computation.3 | loop fusion | flops 64 | bytes 772 | tf_op jit(solution)/shard_map/convert_element_type | solution.py:21
  1.4 0.2 multiply_sine_fusion
  1.6 0.1 broadcast_in_dim.2.lens
  1.7 1.2 %copy.13.w_query = bf16[2048,64]{1,0:T(8,128)(2,1)S(1)} copy(bf16[2048,64]{0,1:T(8,128)(2,1)} %param.9) | data formatting | bytes 524288 | tf_op args[1]
  2.9 0.0 copy-start
  2.9 3.4 %copy-done = bf16[2048,2048]{1,0:T(8,128)(2,1)S(1)} copy-done((bf16[2048,2048]{1,0:T(8,128)(2,1)S(1)}, bf16[2048,2048]{1,0:T(8,128)(2,1)}, u32[]{:S(2)}) %copy-start) | copy-done | bytes 8388632
  6.3 0.0 copy-start.2
  6.3 2.2 %copy-done.2 = bf16[64,256,128]{2,1,0:T(8,128)(2,1)S(1)} copy-done((bf16[64,256,128]{2,1,0:T(8,128)(2,1)S(1)}, bf16[64,256,128]{2,1,0:T(8,128)(2,1)}, u32[]{:S(2)}) %copy-start.2) | copy-done | bytes 4194328
  8.5 0.0 copy-start.3
  8.5 2.2 %copy-done.3 = bf16[64,256,128]{2,1,0:T(8,128)(2,1)S(1)} copy-done((bf16[64,256,128]{2,1,0:T(8,128)(2,1)S(1)}, bf16[64,256,128]{2,1,0:T(8,128)(2,1)}, u32[]{:S(2)}) %copy-start.3) | copy-done | bytes 4194328
  10.7 0.0 copy-start.4
  10.7 1.0 %copy-done.4 = bf16[2048,128]{1,0:T(8,128)(2,1)S(1)} copy-done((bf16[2048,128]{1,0:T(8,128)(2,1)S(1)}, bf16[2048,128]{1,0:T(8,128)(2,1)}, u32[]{:S(2)}) %copy-start.4) | copy-done | bytes 524312
  11.7 0.0 copy-start.5
  11.7 1.0 %copy-done.5 = bf16[2048,128]{1,0:T(8,128)(2,1)S(1)} copy-done((bf16[2048,128]{1,0:T(8,128)(2,1)S(1)}, bf16[2048,128]{1,0:T(8,128)(2,1)}, u32[]{:S(2)}) %copy-start.5) | copy-done | bytes 524312
  12.8 0.0 copy-start.6
  12.8 5.2 %cache_update.1 = (bf16[64,256,128]{2,1,0:T(8,128)(2,1)}, bf16[64,256,128]{2,1,0:T(8,128)(2,1)}) custom-call(s32[64]{0:T(128)S(1)} %get-tuple-element.11.lens, bf16[2048,2048]{1,0:T(8,128)(2,1)S(1)} %copy-done, bf16[2048,128]{1,0:T(8,128)(2,1)S(1)} %copy-done.4, bf16[2048,128]{1,0:T(8,128)(2,1)S(1)} %copy-done.5, f32[64,64]{1,0:T(8,128)S(1)} %get-tuple-element.13.cos, ...), custom_call_target="tpu_custom_call" | custom-call | tf_op jit(solution)/shard_map/cache_update/pallas_call | solution.py:365
  17.9 0.0 copy-done.6
  18.0 0.0 copy-start.1
  18.0 2.2 %copy-done.1 = bf16[64,256,128]{2,1,0:T(8,128)(2,1)S(1)} copy-done((bf16[64,256,128]{2,1,0:T(8,128)(2,1)S(1)}, bf16[64,256,128]{2,1,0:T(8,128)(2,1)}, u32[]{:S(2)}) %copy-start.1) | copy-done | bytes 4194328
  20.1 49.1 %attention_step.1 = bf16[32,32,128]{2,1,0:T(8,128)(2,1)S(1)} custom-call(bf16[2048,2048]{1,0:T(8,128)(2,1)} %hidden.3, bf16[2048,64]{1,0:T(8,128)(2,1)S(1)} %copy.13.w_query, bf16[64,2048]{1,0:T(8,128)(2,1)S(1)} %copy-done.6, bf16[64,256,128]{2,1,0:T(8,128)(2,1)S(1)} %copy-done.1, bf16[64,256,128]{2,1,0:T(8,128)(2,1)} %get-tuple-element.9.v_all, ...), custom_call_target="tpu_custom_call" | custom-call | tf_op jit(solution)/shard_map/attention_step/pallas_call | solution.py:379
  69.3 0.2 reshape.21
  69.5 0.1 copy.14
  69.6 0.9 %copy.15 = bf16[2048,64]{0,1:T(8,128)(2,1)} copy(bf16[2048,64]{1,0:T(8,128)(2,1)S(1)} %bitcast.3) | data formatting | bytes 524288
  (1 shorter events, 0.0 us)
Async XLA Ops:
  2.9 3.4 %copy-start = (bf16[2048,2048]{1,0:T(8,128)(2,1)S(1)}, bf16[2048,2048]{1,0:T(8,128)(2,1)}, u32[]{:S(2)}) copy-start(bf16[2048,2048]{1,0:T(8,128)(2,1)} %hidden.3) | copy-start | bytes 25165828
  6.3 2.2 %copy-start.2 = (bf16[64,256,128]{2,1,0:T(8,128)(2,1)S(1)}, bf16[64,256,128]{2,1,0:T(8,128)(2,1)}, u32[]{:S(2)}) copy-start(bf16[64,256,128]{2,1,0:T(8,128)(2,1)} %k_in.1) | copy-start | bytes 12582916
  8.5 2.2 %copy-start.3 = (bf16[64,256,128]{2,1,0:T(8,128)(2,1)S(1)}, bf16[64,256,128]{2,1,0:T(8,128)(2,1)}, u32[]{:S(2)}) copy-start(bf16[64,256,128]{2,1,0:T(8,128)(2,1)} %v_in.1) | copy-start | bytes 12582916
  10.7 1.0 %copy-start.4 = (bf16[2048,128]{1,0:T(8,128)(2,1)S(1)}, bf16[2048,128]{1,0:T(8,128)(2,1)}, u32[]{:S(2)}) copy-start(bf16[2048,128]{1,0:T(8,128)(2,1)} %w_key.1) | copy-start | bytes 1572868
  11.7 1.0 %copy-start.5 = (bf16[2048,128]{1,0:T(8,128)(2,1)S(1)}, bf16[2048,128]{1,0:T(8,128)(2,1)}, u32[]{:S(2)}) copy-start(bf16[2048,128]{1,0:T(8,128)(2,1)} %w_value.1) | copy-start | bytes 1572868
  12.8 5.2 %copy-start.6 = (bf16[64,2048]{1,0:T(8,128)(2,1)S(1)}, bf16[64,2048]{1,0:T(8,128)(2,1)}, u32[]{:S(2)}) copy-start(bf16[64,2048]{1,0:T(8,128)(2,1)} %w_out.1) | copy-start | bytes 786436
  18.0 2.2 %copy-start.1 = (bf16[64,256,128]{2,1,0:T(8,128)(2,1)S(1)}, bf16[64,256,128]{2,1,0:T(8,128)(2,1)}, u32[]{:S(2)}) copy-start(bf16[64,256,128]{2,1,0:T(8,128)(2,1)} %get-tuple-element.8.k_all) | copy-start | bytes 12582916

commit v2 on v0

v2 whole, which is shorter than its diff:
```python
import functools
import math

import jax
import jax.numpy as jnp
import numpy as np
from jax import lax
from jax.experimental import pallas as pl
from jax.experimental.pallas import tpu as pltpu
from jax.sharding import PartitionSpec as P

F32, BF16 = jnp.float32, jnp.bfloat16
MESH = pl.DeviceIdType.MESH
O_STEPS = 4
SUB = 8
VMEM_LIMIT = 55 << 20


def step_kernel(side, hidden, wq_turned, w_key, w_value, w_out, k_in, v_in, lengths, freq, y_out, k_buf, v_buf,
                lens, lens_f, h_buf, wq_buf, wk_buf, wv_buf, wo_buf, w_buf, k_new, v_new,
                q_send, q_recv, q_rows, s_rows, p_rows, o_rows, o_buf, y_send, y_recv,
                h_sem, small_sem, wo_sem, k_sem, v_sem,
                q_ssem, q_rsem, w_ssem, w_rsem, w_xsem, o_ssem, o_rsem, y_ssem, y_rsem):
    rows, seq, dim = k_in.shape
    half = dim // 2
    pack = rows // 2
    group = 2 * side * side
    heads = group // 2
    cols = w_buf.shape[1]
    me = lax.axis_index("tp")
    core = lax.rem(me, 2)
    chip = me // 2
    x = lax.rem(chip, side)
    y = chip // side

    def index(xx, yy, cc):
        return (lax.rem(yy, side) * side + lax.rem(xx, side)) * 2 + cc

    def remote(src, dst, ssem, rsem, target):
        return pltpu.make_async_remote_copy(src_ref=src, dst_ref=dst, send_sem=ssem, recv_sem=rsem,
                                            device_id={"tp": target}, device_id_type=MESH)

    def wait_recv(ref, rsem):
        remote(ref, ref, q_ssem, rsem, me).wait_recv()

    def wait_send(ref, ssem):
        remote(ref, ref, ssem, q_rsem, me).wait_send()

    block = rows * 2 * side
    ydest = [lax.rem(y + d, side) for d in (2, 1, 3, 0)]

    def h_part(yy):
        return pl.ds(pl.multiple_of(yy * block, block), block)

    small = [pltpu.make_async_copy(src, dst, small_sem.at[i]) for i, (src, dst) in enumerate(
        ((wq_turned, wq_buf), (lengths, lens), (w_key, wk_buf), (w_value, wv_buf)))]
    h_copies = [pltpu.make_async_copy(hidden.at[h_part(yy)], h_buf.at[h_part(yy)], h_sem.at[i]) for i, yy in enumerate(ydest)]
    wo_copies = [pltpu.make_async_copy(w_out.at[:, pl.ds(i * cols, cols)], wo_buf.at[i], wo_sem.at[i]) for i in range(side)]
    step_rows = rows // O_STEPS
    kv_copies = []
    for k in range(O_STEPS):
        part = pl.ds(k * step_rows, step_rows)
        kv_copies.append((pltpu.make_async_copy(k_in.at[part], k_buf.at[part], k_sem.at[k]),
                          pltpu.make_async_copy(v_in.at[part], v_buf.at[part], v_sem.at[k])))
    small[0].start()
    h_copies[0].start()
    h_copies[1].start()
    small[1].start()

    barrier = pltpu.get_barrier_semaphore()
    peers = [(lax.rem(chip + i, heads)) * 2 + c for i in range(1, heads) for c in range(2)] + [chip * 2 + (1 - core)]
    for peer in peers:
        pl.semaphore_signal(barrier, inc=1, device_id={"tp": peer}, device_id_type=MESH)

    with jax.named_scope("wait_wq"):
        small[0].wait()
    wq = wq_buf[...].T
    own = x * 2 + core
    for i, yy in enumerate(ydest):
        with jax.named_scope("wait_h"):
            h_copies[i].wait()
        if i + 2 < side:
            h_copies[i + 2].start()
        if i == 1:
            for copy in wo_copies + small[2:]:
                copy.start()
        if i == 2:
            for k in range(O_STEPS // 2):
                for copy in kv_copies[k]:
                    copy.start()
        q_val = jnp.dot(h_buf[h_part(yy), :], wq, preferred_element_type=F32).astype(BF16)
        q_val = q_val.reshape(2 * side, 2, pack, half)
        q_send[pl.ds(i * 2 * side, 2 * side)] = jnp.concatenate([q_val[:, 0], q_val[:, 1]], axis=-1)
        if i == 0:
            with jax.named_scope("barrier"):
                pl.semaphore_wait(barrier, len(peers))

        def send_q(j, carry, i=i, yy=yy):
            slot = lax.rem(own + 1 + j, 2 * side)
            remote(q_send.at[i * 2 * side + slot], q_recv.at[me], q_ssem, q_rsem, yy * 2 * side + slot).start()
            return carry

        lax.fori_loop(0, 2 * side if i < side - 1 else 2 * side - 1, send_q, 0)
    q_recv[me] = q_send[(side - 1) * 2 * side + own]
    for k in range(O_STEPS // 2, O_STEPS):
        for copy in kv_copies[k]:
            copy.start()

    def w_slot(t):
        return w_buf.at[pl.ds(pl.multiple_of(t * half, half), half)]

    left, right, other = index(x + side - 1, y, core), index(x + 1, y, core), chip * 2 + (1 - core)
    n_w = [0]

    def send_w(src, t, target):
        n_w[0] += 1
        remote(src, w_slot(t), w_ssem, w_rsem.at[t], target).start()

    def give_w(src, t):
        n_w[0] += 1
        remote(src, w_slot(t), w_ssem, w_xsem, other).start()

    def wait_w(t):
        wait_recv(w_slot(t), w_rsem.at[t])

    with jax.named_scope("send_w"):
        for copy in wo_copies:
            copy.wait()
        for d in (1, 3, 2):
            send_w(wo_buf.at[lax.rem(y + d, side)], me, index(x, y + d, core))
        for target in (right, left):
            send_w(wo_buf.at[y], me, target)
        give_w(wo_buf.at[y], me)
        w_buf[pl.ds(pl.multiple_of(me * half, half), half)] = wo_buf[y]

    def forward_column(d):
        t = index(x, y + d, core)
        wait_w(t)
        for target in (right, left):
            send_w(w_slot(t), t, target)
        give_w(w_slot(t), t)

    def relay_right(d):
        t = index(x + side - 1, y + d, core)
        wait_w(t)
        send_w(w_slot(t), t, right)
        give_w(w_slot(t), t)

    def relay_left(d):
        t = index(x + 1, y + d, core)
        wait_w(t)
        send_w(w_slot(t), t, left)
        give_w(w_slot(t), t)

    def pass_on(xx, d):
        t = index(xx, y + d, core)
        wait_w(t)
        give_w(w_slot(t), t)

    with jax.named_scope("tables"):
        small[1].wait()

        def spread(r, carry):
            lens_f[pl.ds(r, 1), :] = jnp.full((1, dim), lens[me * rows + r].astype(F32))
            return carry

        lax.fori_loop(0, rows, spread, 0, unroll=8)
        angles = lens_f[...] * freq[...]
        cos, sin = jnp.cos(angles), jnp.sin(angles)
        low = lax.broadcasted_iota(jnp.int32, (rows, dim), 1) < half
        low_pack = lax.broadcasted_iota(jnp.int32, (pack, dim), 1) < half
        c_pack = jnp.where(low_pack, cos[:pack], cos[pack:])
        s_pack = jnp.where(low_pack, sin[:pack], sin[pack:])
        small[2].wait()
        small[3].wait()
        h_own = h_buf[pl.ds(pl.multiple_of(me * rows, rows), rows), :]
        key = jnp.dot(h_own, wk_buf[...], preferred_element_type=F32).astype(BF16).astype(F32)
        turned_key = pltpu.roll(key, half, 1)
        k_new[...] = jnp.where(low, key * cos - turned_key * sin, key * cos + turned_key * sin)
        v_new[...] = jnp.dot(h_own, wv_buf[...], preferred_element_type=F32)
    slot_rows = lax.broadcasted_iota(jnp.int32, (seq, dim), 0).astype(F32).astype(BF16)
    with jax.named_scope("patch"):
        for k in range(O_STEPS):
            for copy in kv_copies[k]:
                copy.wait()

            def patch(j, carry, k=k):
                r = k * step_rows + j
                here = slot_rows == lens_f[pl.ds(r, 1), :].astype(BF16)
                k_buf[r] = jnp.where(here, k_new[pl.ds(r, 1), :].astype(BF16), k_buf[r])
                v_buf[r] = jnp.where(here, v_new[pl.ds(r, 1), :].astype(BF16), v_buf[r])
                return carry

            lax.fori_loop(0, step_rows, patch, 0)

    with jax.named_scope("wait_q"):
        wait_recv(q_recv.at[pl.ds(0, group - 1)], q_rsem)
    with jax.named_scope("rope"):
        for i in range(heads):
            p1, p2 = q_recv[2 * i].astype(F32), q_recv[2 * i + 1].astype(F32)
            r1, r2 = p1 * c_pack - p2 * s_pack, p2 * c_pack + p1 * s_pack
            q_rows[pl.ds(i, pack, stride=heads), :] = jnp.where(low_pack, r1, pltpu.roll(r2, half, 1))
            q_rows[pl.ds(pack * heads + i, pack, stride=heads), :] = jnp.where(low_pack, pltpu.roll(r1, half, 1), r2)

    scale = dim ** -0.5
    slots = lax.broadcasted_iota(jnp.int32, (heads, seq), 1).astype(F32)
    up, down = index(x, y + 1, core), index(x, y + side - 1, core)
    y_up, y_down, y_far = lax.rem(y + 1, side), lax.rem(y + side - 1, side), lax.rem(y + 2, side)

    def send_o(yy, k, target):
        piece = o_buf.at[yy * O_STEPS + k]
        remote(piece, piece, o_ssem, o_rsem.at[yy, k], target).start()

    def wait_o(yy, k):
        wait_recv(o_buf.at[yy * O_STEPS + k], o_rsem.at[yy, k])

    def relay_o(k):
        if k % 2 == 0:
            wait_o(y_down, k)
            send_o(y_down, k, up)
        else:
            wait_o(y_up, k)
            send_o(y_up, k, down)

    def score(k, part):
        r = k * step_rows + part
        q_row = q_rows[pl.ds(r * heads, heads), :].astype(BF16)
        scores = lax.dot_general(q_row, k_buf[r], (((1,), (1,)), ((), ())), preferred_element_type=F32) * scale
        last = jnp.concatenate([lens_f[pl.ds(r, 1), :]] * (seq // dim), axis=1)
        s_rows[pl.ds(part * heads, heads), :] = jnp.where(slots <= last, scores, -1e30)

    def attend(k):
        for part in range(step_rows):
            score(k, part)
        for first in range(0, step_rows, SUB):
            span = pl.ds(first * heads, SUB * heads)
            scores = s_rows[span, :]
            weights = jnp.exp(scores - jnp.max(scores, axis=1, keepdims=True))
            p_rows[span, :] = weights.astype(BF16)
            total = jnp.sum(weights, axis=1, keepdims=True)
            for u in range(SUB):
                part = first + u
                summed = jnp.dot(p_rows[pl.ds(part * heads, heads), :], v_buf[k * step_rows + part], preferred_element_type=F32)
                o_rows[pl.ds(part * heads, heads), :] = summed / total[u * heads:(u + 1) * heads]
        for i in range(heads):
            o_buf[y * O_STEPS + k, i] = o_rows[pl.ds(i, step_rows, stride=heads), :].astype(BF16)
        send_o(y, k, up)
        send_o(y, k, down)

    with jax.named_scope("attend0"):
        attend(0)
    with jax.named_scope("column"):
        for d in (1, 3, 2):
            forward_column(d)
    with jax.named_scope("attend1"):
        attend(1)
    with jax.named_scope("relay1"):
        relay_right(0)
        pass_on(x + 1, 0)
    with jax.named_scope("attend2"):
        attend(2)
    with jax.named_scope("relay2"):
        relay_o(0)
    with jax.named_scope("attend3"):
        attend(3)
    with jax.named_scope("relay3"):
        relay_o(1)
        relay_right(1)
        relay_left(3)
        relay_left(2)
    with jax.named_scope("relay4"):
        relay_o(2)
        relay_o(3)
    with jax.named_scope("pass_on"):
        pass_on(x + side - 1, 3)
        pass_on(x + side - 1, 2)
        pass_on(x + 1, 1)
    with jax.named_scope("wait_w_far"):
        for d in (0, 1, 3, 2):
            pass_on(x + 2, d)
    with jax.named_scope("wait_w_other"):
        wait_recv(w_buf.at[pl.ds(0, heads * half)], w_xsem)

    n_y = [0]

    def project(yy):
        n = n_y[0]
        n_y[0] += 1
        lhs = jnp.concatenate([o_buf[pl.ds(yy * O_STEPS, O_STEPS), i].reshape(rows, dim) for i in range(heads)], axis=1)
        res = jnp.dot(lhs, w_buf[...], preferred_element_type=F32)
        row_owner = index(x, yy, core)
        for slot in range(0, 2 * side, 2):
            turned = res[:, slot * half:(slot + 2) * half].T.astype(BF16)
            for c in range(2):
                part = turned[c * half:(c + 1) * half]
                y_send[n * 2 * side + slot + c] = jnp.concatenate([part[:half // 2], part[half // 2:]], axis=1)

        def send_y(j, carry):
            slot = lax.rem(own + 1 + j, 2 * side)
            remote(y_send.at[n * 2 * side + slot], y_recv.at[row_owner], y_ssem, y_rsem, y * 2 * side + slot).start()
            return carry

        lax.fori_loop(0, 2 * side - 1, send_y, 0)
        y_recv[row_owner] = y_send[n * 2 * side + own]

    with jax.named_scope("project0"):
        project(y)
    with jax.named_scope("wait_o_up"):
        wait_o(y_up, 0)
        wait_o(y_up, 2)
    with jax.named_scope("project1"):
        project(y_up)
    with jax.named_scope("wait_o_down"):
        wait_o(y_down, 1)
        wait_o(y_down, 3)
    with jax.named_scope("project2"):
        project(y_down)
    with jax.named_scope("wait_o_far"):
        for k in range(O_STEPS):
            wait_o(y_far, k)
    with jax.named_scope("project3"):
        project(y_far)
    with jax.named_scope("drain"):
        wait_send(q_send.at[pl.ds(0, group - 1)], q_ssem)
        wait_send(w_buf.at[pl.ds(0, n_w[0] * half)], w_ssem)
        wait_send(o_buf.at[pl.ds(0, 3 * O_STEPS)], o_ssem)
    with jax.named_scope("wait_y"):
        wait_recv(y_recv.at[pl.ds(0, side * (2 * side - 1))], y_rsem)
    with jax.named_scope("finish"):
        for i in range(heads):
            a, b = y_recv[2 * i], y_recv[2 * i + 1]
            two_rows = pl.ds(i * 2 * rows, 2 * rows)
            y_out[pl.ds(0, half // 2), two_rows] = jnp.concatenate([a[:, :rows], b[:, :rows]], axis=1)
            y_out[pl.ds(half // 2, half // 2), two_rows] = jnp.concatenate([a[:, rows:], b[:, rows:]], axis=1)
        wait_send(y_send.at[pl.ds(0, side * (2 * side - 1))], y_ssem)


def solution(mesh):
    group = mesh.shape["tp"]
    side = math.isqrt(group // 2)
    cache_spec = P(("dp", "tp"), None, None)
    vmem, hbm = pl.BlockSpec(memory_space=pltpu.VMEM), pl.BlockSpec(memory_space=pltpu.HBM)
    dma = pltpu.SemaphoreType.DMA

    def local_step(hidden, w_query, w_key, w_value, w_out, k_cache, v_cache, lengths):
        rows, seq, dim = k_cache.shape
        batch, embed = hidden.shape
        half = dim // 2
        heads = group * w_query.shape[1] // dim
        cols = w_out.shape[1] // side
        freq = (10000.0 ** (-(np.arange(half) * 2.0) / dim)).astype(np.float32)
        freq = jnp.asarray(np.concatenate([freq, freq])[None, :])
        cache_shape = pltpu.VMEM(k_cache.shape, k_cache.dtype)
        y_turned, k_out, v_out = pl.pallas_call(
            functools.partial(step_kernel, side),
            out_shape=(pltpu.VMEM((w_out.shape[1] // group, batch), BF16), cache_shape, cache_shape),
            in_specs=[hbm] * 8 + [vmem],
            out_specs=(vmem, vmem, vmem),
            scratch_shapes=[
                pltpu.SMEM((batch,), jnp.int32), pltpu.VMEM((rows, dim), F32),
                pltpu.VMEM((batch, embed), BF16), pltpu.VMEM((half, embed), BF16),
                pltpu.VMEM((embed, dim), BF16), pltpu.VMEM((embed, dim), BF16),
                pltpu.VMEM((side, half, cols), BF16), pltpu.VMEM((group * half, cols), BF16),
                pltpu.VMEM((rows, dim), F32), pltpu.VMEM((rows, dim), F32),
                pltpu.VMEM((group, rows // 2, dim), BF16), pltpu.VMEM((group, rows // 2, dim), BF16),
                pltpu.VMEM((rows * heads, dim), F32), pltpu.VMEM((rows // O_STEPS * heads, seq), F32),
                pltpu.VMEM((rows // O_STEPS * heads, seq), BF16), pltpu.VMEM((rows // O_STEPS * heads, dim), F32),
                pltpu.VMEM((side * O_STEPS, heads, rows // O_STEPS, dim), BF16),
                pltpu.VMEM((group, rows // 2, dim), BF16), pltpu.VMEM((group, rows // 2, dim), BF16),
                dma((side,)), dma((4,)), dma((side,)), dma((O_STEPS,)), dma((O_STEPS,)),
                dma, dma, dma, dma((group,)), dma, dma, dma((side, O_STEPS)), dma, dma,
            ],
            compiler_params=pltpu.CompilerParams(collective_id=0, has_side_effects=True, vmem_limit_bytes=VMEM_LIMIT),
            name="attention_step",
        )(hidden, w_query.T, w_key, w_value, w_out, k_cache, v_cache, lengths, freq)
        return y_turned.T, k_out, v_out

    return jax.shard_map(
        local_step,
        mesh=mesh,
        in_specs=(P("dp", None), P(None, "tp"), P(), P(), P("tp", None), cache_spec, cache_spec, P("dp")),
        out_specs=(P("dp", "tp"), cache_spec, cache_spec),
        check_vma=False,
    )
```

time: 155 us -> 41.8 us (0.27)
  waiting for transfers between devices: 81 us -> 0 us
  Pallas kernels: 0 us -> 36.3 us
  matrix products: 18.5 us -> 0 us
  blocking collectives: 14.9 us -> 0 us
  between operations: 14.3 us -> 0.64 us
  other arithmetic: 11.6 us -> 0 us
  starting transfers between devices: 9.2 us -> 0 us
    reduce_scatter x1 -> x0, waiting for transfers between devices: 80.9 us -> none  [local_step(): y_local = lax.psum_scatter(y_part, 'tp', scatter_dimension=1, tiled=True)]
    pallas_call x0 -> x1, Pallas kernels: none -> 36.3 us  [local_step(): pl.pallas_call(functools.partial(step_kernel, side), out_shape=(pltpu.VME...]
    dot_general x6 -> x0, matrix products: 18.5 us -> none  [the longest x1 6.09 us: local_step(): jnp.dot(hidden, w_query, preferred_element_type=jnp.float32)]
    all_to_all x1 -> x0, blocking collectives: 14.9 us -> none  [local_step(): lax.all_to_all(attn_out.reshape(rows_dev, num_heads * head_dim), 'tp', 1,...]
    select_n x1 -> x0, other arithmetic: 9.79 us -> none  [local_step(): k_out = jnp.where(new_slot, k_rot[:, None, :], k_cache)]
    all_to_all x1 -> x0, starting transfers between devices: 9.14 us -> none  [local_step(): q_rows = lax.all_to_all(q_cols, 'tp', 0, 1, tiled=True)]
    unnamed x14 -> x3, local copies, waits for them, and re-layouts: 2.78 us -> 4.73 us
    all_to_all x6 -> x0, local copies, waits for them, and re-layouts: 1.88 us -> none  [the longest x4 1.17 us: local_step(): lax.all_to_all(attn_out.reshape(rows_dev, num_heads * head_dim), 'tp', 1,...]
  transfers between devices with their start and end apart: 2 -> 0, of which waited for: 1 -> 0; matrix products, arithmetic and copies ran while one was open for 9% -> 0% of each run, Pallas kernels for 0% -> 0%
where the time goes in v2:
time: 41.8 us; the launch traced here: 41.7 us
  Pallas kernels  36.3 us (87%)
  local copies, waits for them, and re-layouts  4.73 us (11%)
  between operations  0.64 us (2%)
    pallas_call x1, Pallas kernels, local_step(): pl.pallas_call(functools.partial(step_kernel, side), out_shape=(pltpu.VME...  36.3 us
    unnamed x3, local copies, waits for them, and re-layouts  4.73 us

profile of v2, /device:TPU:97, one launch (start us, length us, event | category | flops | bytes accessed | tf_op | source)
XLA Modules:
  0.0 41.7 jit_solution(1858654672488635127)
XLA Ops:
  0.6 36.3 %attention_step.1 = (bf16[64,2048]{1,0:T(8,128)(2,1)S(1)}, bf16[64,256,128]{2,1,0:T(8,128)(2,1)S(1)}, bf16[64,256,128]{2,1,0:T(8,128)(2,1)S(1)}) custom-call(bf16[2048,2048]{1,0:T(8,128)(2,1)} %hidden.1, bf16[64,2048]{1,0:T(8,128)(2,1)} %bitcast.3, bf16[2048,128]{1,0:T(8,128)(2,1)} %w_key.1, bf16[2048,128]{1,0:T(8,128)(2,1)} %w_value.1, ...), custom_call_target="tpu_custom_call" | custom-call | tf_op jit(solution)/shard_map/attention_step/pallas_call | solution.py:354
  37.0 0.7 %copy.15 = bf16[2048,64]{0,1:T(8,128)(2,1)} copy(bf16[2048,64]{0,1:T(8,128)(2,1)S(1)} %bitcast.2) | data formatting | bytes 524288
  37.7 2.0 %copy.16 = bf16[64,256,128]{2,1,0:T(8,128)(2,1)} copy(bf16[64,256,128]{2,1,0:T(8,128)(2,1)S(1)} %get-tuple-element.10) | data formatting | bytes 8388608
  39.7 2.0 %copy.17 = bf16[64,256,128]{2,1,0:T(8,128)(2,1)} copy(bf16[64,256,128]{2,1,0:T(8,128)(2,1)S(1)} %get-tuple-element.11) | data formatting | bytes 8388608

commit v3 on v2

--- a/solution.py
+++ b/solution.py
@@ -16,8 +16,8 @@
 VMEM_LIMIT = 55 << 20
 
 
-def step_kernel(side, hidden, wq_turned, w_key, w_value, w_out, k_in, v_in, lengths, freq, y_out, k_buf, v_buf,
-                lens, lens_f, h_buf, wq_buf, wk_buf, wv_buf, wo_buf, w_buf, k_new, v_new,
+def step_kernel(side, hidden, wq_turned, w_key, w_value, w_out, k_in, v_in, lengths, freq_in, y_out, k_buf, v_buf,
+                lens, freq, lens_f, h_buf, wq_buf, wk_buf, wv_buf, wo_buf, w_buf, k_new, v_new,
                 q_send, q_recv, q_rows, s_rows, p_rows, o_rows, o_buf, y_send, y_recv,
                 h_sem, small_sem, wo_sem, k_sem, v_sem,
                 q_ssem, q_rsem, w_ssem, w_rsem, w_xsem, o_ssem, o_rsem, y_ssem, y_rsem):
@@ -53,7 +53,7 @@
         return pl.ds(pl.multiple_of(yy * block, block), block)
 
     small = [pltpu.make_async_copy(src, dst, small_sem.at[i]) for i, (src, dst) in enumerate(
-        ((wq_turned, wq_buf), (lengths, lens), (w_key, wk_buf), (w_value, wv_buf)))]
+        ((wq_turned, wq_buf), (lengths, lens), (w_key, wk_buf), (w_value, wv_buf), (freq_in, freq)))]
     h_copies = [pltpu.make_async_copy(hidden.at[h_part(yy)], h_buf.at[h_part(yy)], h_sem.at[i]) for i, yy in enumerate(ydest)]
     wo_copies = [pltpu.make_async_copy(w_out.at[:, pl.ds(i * cols, cols)], wo_buf.at[i], wo_sem.at[i]) for i in range(side)]
     step_rows = rows // O_STEPS
@@ -64,13 +64,45 @@
                           pltpu.make_async_copy(v_in.at[part], v_buf.at[part], v_sem.at[k])))
     small[0].start()
     h_copies[0].start()
+    for copy in wo_copies:
+        copy.start()
     h_copies[1].start()
     small[1].start()
+    small[4].start()
 
     barrier = pltpu.get_barrier_semaphore()
     peers = [(lax.rem(chip + i, heads)) * 2 + c for i in range(1, heads) for c in range(2)] + [chip * 2 + (1 - core)]
     for peer in peers:
         pl.semaphore_signal(barrier, inc=1, device_id={"tp": peer}, device_id_type=MESH)
+
+    def w_slot(t):
+        return w_buf.at[pl.ds(pl.multiple_of(t * half, half), half)]
+
+    left, right, other = index(x + side - 1, y, core), index(x + 1, y, core), chip * 2 + (1 - core)
+    n_w = [0]
+
+    def send_w(src, t, target):
+        n_w[0] += 1
+        remote(src, w_slot(t), w_ssem, w_rsem.at[t], target).start()
+
+    def give_w(src, t):
+        n_w[0] += 1
+        remote(src, w_slot(t), w_ssem, w_xsem, other).start()
+
+    def wait_w(t):
+        wait_recv(w_slot(t), w_rsem.at[t])
+
+    def first_w():
+        for copy in wo_copies:
+            copy.wait()
+        for d in (1, 3, 2):
+            send_w(wo_buf.at[lax.rem(y + d, side)], me, index(x, y + d, core))
+
+    def own_w():
+        for target in (right, left):
+            send_w(wo_buf.at[y], me, target)
+        give_w(wo_buf.at[y], me)
+        w_buf[pl.ds(pl.multiple_of(me * half, half), half)] = wo_buf[y]
 
     with jax.named_scope("wait_wq"):
         small[0].wait()
@@ -82,15 +114,17 @@
         if i + 2 < side:
             h_copies[i + 2].start()
         if i == 1:
-            for copy in wo_copies + small[2:]:
+            for copy in small[2:4]:
                 copy.start()
         if i == 2:
             for k in range(O_STEPS // 2):
                 for copy in kv_copies[k]:
                     copy.start()
-        q_val = jnp.dot(h_buf[h_part(yy), :], wq, preferred_element_type=F32).astype(BF16)
-        q_val = q_val.reshape(2 * side, 2, pack, half)
-        q_send[pl.ds(i * 2 * side, 2 * side)] = jnp.concatenate([q_val[:, 0], q_val[:, 1]], axis=-1)
+        for part in range(2):
+            some = pl.ds(pl.multiple_of(yy * block + part * (block // 2), block // 2), block // 2)
+            q_val = jnp.dot(h_buf[some, :], wq, preferred_element_type=F32).astype(BF16)
+            q_val = q_val.reshape(side, 2, pack, half)
+            q_send[pl.ds(i * 2 * side + part * side, side)] = jnp.concatenate([q_val[:, 0], q_val[:, 1]], axis=-1)
         if i == 0:
             with jax.named_scope("barrier"):
                 pl.semaphore_wait(barrier, len(peers))
@@ -101,37 +135,13 @@
             return carry
 
         lax.fori_loop(0, 2 * side if i < side - 1 else 2 * side - 1, send_q, 0)
+        if i == side - 2:
+            first_w()
+    own_w()
     q_recv[me] = q_send[(side - 1) * 2 * side + own]
     for k in range(O_STEPS // 2, O_STEPS):
         for copy in kv_copies[k]:
             copy.start()
-
-    def w_slot(t):
-        return w_buf.at[pl.ds(pl.multiple_of(t * half, half), half)]
-
-    left, right, other = index(x + side - 1, y, core), index(x + 1, y, core), chip * 2 + (1 - core)
-    n_w = [0]
-
-    def send_w(src, t, target):
-        n_w[0] += 1
-        remote(src, w_slot(t), w_ssem, w_rsem.at[t], target).start()
-
-    def give_w(src, t):
-        n_w[0] += 1
-        remote(src, w_slot(t), w_ssem, w_xsem, other).start()
-
-    def wait_w(t):
-        wait_recv(w_slot(t), w_rsem.at[t])
-
-    with jax.named_scope("send_w"):
-        for copy in wo_copies:
-            copy.wait()
-        for d in (1, 3, 2):
-            send_w(wo_buf.at[lax.rem(y + d, side)], me, index(x, y + d, core))
-        for target in (right, left):
-            send_w(wo_buf.at[y], me, target)
-        give_w(wo_buf.at[y], me)
-        w_buf[pl.ds(pl.multiple_of(me * half, half), half)] = wo_buf[y]
 
     def forward_column(d):
         t = index(x, y + d, core)
@@ -159,6 +169,7 @@
 
     with jax.named_scope("tables"):
         small[1].wait()
+        small[4].wait()
 
         def spread(r, carry):
             lens_f[pl.ds(r, 1), :] = jnp.full((1, dim), lens[me * rows + r].astype(F32))
@@ -254,27 +265,26 @@
             forward_column(d)
     with jax.named_scope("attend1"):
         attend(1)
-    with jax.named_scope("relay1"):
+    with jax.named_scope("relay0"):
         relay_right(0)
         pass_on(x + 1, 0)
     with jax.named_scope("attend2"):
         attend(2)
+        attend(3)
+    with jax.named_scope("relay1"):
+        relay_right(1)
+        relay_left(3)
     with jax.named_scope("relay2"):
         relay_o(0)
-    with jax.named_scope("attend3"):
-        attend(3)
+        relay_left(2)
     with jax.named_scope("relay3"):
         relay_o(1)
-        relay_right(1)
-        relay_left(3)
-        relay_left(2)
+        pass_on(x + side - 1, 3)
+        pass_on(x + side - 1, 2)
+        pass_on(x + 1, 1)
     with jax.named_scope("relay4"):
         relay_o(2)
         relay_o(3)
-    with jax.named_scope("pass_on"):
-        pass_on(x + side - 1, 3)
-        pass_on(x + side - 1, 2)
-        pass_on(x + 1, 1)
     with jax.named_scope("wait_w_far"):
         for d in (0, 1, 3, 2):
             pass_on(x + 2, d)
@@ -283,42 +293,39 @@
 
     n_y = [0]
 
-    def project(yy):
-        n = n_y[0]
-        n_y[0] += 1
-        lhs = jnp.concatenate([o_buf[pl.ds(yy * O_STEPS, O_STEPS), i].reshape(rows, dim) for i in range(heads)], axis=1)
-        res = jnp.dot(lhs, w_buf[...], preferred_element_type=F32)
-        row_owner = index(x, yy, core)
-        for slot in range(0, 2 * side, 2):
-            turned = res[:, slot * half:(slot + 2) * half].T.astype(BF16)
-            for c in range(2):
-                part = turned[c * half:(c + 1) * half]
-                y_send[n * 2 * side + slot + c] = jnp.concatenate([part[:half // 2], part[half // 2:]], axis=1)
-
-        def send_y(j, carry):
-            slot = lax.rem(own + 1 + j, 2 * side)
-            remote(y_send.at[n * 2 * side + slot], y_recv.at[row_owner], y_ssem, y_rsem, y * 2 * side + slot).start()
-            return carry
-
-        lax.fori_loop(0, 2 * side - 1, send_y, 0)
-        y_recv[row_owner] = y_send[n * 2 * side + own]
-
-    with jax.named_scope("project0"):
-        project(y)
-    with jax.named_scope("wait_o_up"):
+    def project(*sources):
+        lhs = [jnp.concatenate([o_buf[pl.ds(yy * O_STEPS, O_STEPS), i].reshape(rows, dim) for i in range(heads)], axis=1)
+               for yy in sources]
+        res = jnp.dot(jnp.concatenate(lhs, axis=0), w_buf[...], preferred_element_type=F32)
+        for m, yy in enumerate(sources):
+            n = n_y[0]
+            n_y[0] += 1
+            row_owner = index(x, yy, core)
+            for slot in range(0, 2 * side, 2):
+                turned = res[m * rows:(m + 1) * rows, slot * half:(slot + 2) * half].T.astype(BF16)
+                for c in range(2):
+                    part = turned[c * half:(c + 1) * half]
+                    y_send[n * 2 * side + slot + c] = jnp.concatenate([part[:half // 2], part[half // 2:]], axis=1)
+
+            def send_y(j, carry, n=n, row_owner=row_owner):
+                slot = lax.rem(own + 1 + j, 2 * side)
+                remote(y_send.at[n * 2 * side + slot], y_recv.at[row_owner], y_ssem, y_rsem, y * 2 * side + slot).start()
+                return carry
+
+            lax.fori_loop(0, 2 * side - 1, send_y, 0)
+            y_recv[row_owner] = y_send[n * 2 * side + own]
+
+    with jax.named_scope("wait_o_near"):
         wait_o(y_up, 0)
         wait_o(y_up, 2)
-    with jax.named_scope("project1"):
-        project(y_up)
-    with jax.named_scope("wait_o_down"):
         wait_o(y_down, 1)
         wait_o(y_down, 3)
-    with jax.named_scope("project2"):
-        project(y_down)
+    with jax.named_scope("project_near"):
+        project(y, y_up, y_down)
     with jax.named_scope("wait_o_far"):
         for k in range(O_STEPS):
             wait_o(y_far, k)
-    with jax.named_scope("project3"):
+    with jax.named_scope("project_far"):
         project(y_far)
     with jax.named_scope("drain"):
         wait_send(q_send.at[pl.ds(0, group - 1)], q_ssem)
@@ -335,6 +342,21 @@
         wait_send(y_send.at[pl.ds(0, side * (2 * side - 1))], y_ssem)
 
 
+def write_kernel(y_in, k_in, v_in, y_out, k_out, v_out, sems):
+    rows = k_in.shape[0]
+    part_rows = rows // O_STEPS
+    copies = []
+    for src, dst in ((k_in, k_out), (v_in, v_out)):
+        for j in range(O_STEPS):
+            part = pl.ds(j * part_rows, part_rows)
+            copies.append(pltpu.make_async_copy(src.at[part], dst.at[part], sems.at[len(copies)]))
+    copies.append(pltpu.make_async_copy(y_in, y_out, sems.at[len(copies)]))
+    for copy in copies:
+        copy.start()
+    for copy in copies:
+        copy.wait()
+
+
 def solution(mesh):
     group = mesh.shape["tp"]
     side = math.isqrt(group // 2)
@@ -351,13 +373,14 @@
         freq = (10000.0 ** (-(np.arange(half) * 2.0) / dim)).astype(np.float32)
         freq = jnp.asarray(np.concatenate([freq, freq])[None, :])
         cache_shape = pltpu.VMEM(k_cache.shape, k_cache.dtype)
-        y_turned, k_out, v_out = pl.pallas_call(
+        y_shape = ((w_out.shape[1] // group, batch), BF16)
+        y_turned, k_new, v_new = pl.pallas_call(
             functools.partial(step_kernel, side),
-            out_shape=(pltpu.VMEM((w_out.shape[1] // group, batch), BF16), cache_shape, cache_shape),
-            in_specs=[hbm] * 8 + [vmem],
+            out_shape=(pltpu.VMEM(*y_shape), cache_shape, cache_shape),
+            in_specs=[hbm] * 9,
             out_specs=(vmem, vmem, vmem),
             scratch_shapes=[
-                pltpu.SMEM((batch,), jnp.int32), pltpu.VMEM((rows, dim), F32),
+                pltpu.SMEM((batch,), jnp.int32), pltpu.VMEM((1, dim), F32), pltpu.VMEM((rows, dim), F32),
                 pltpu.VMEM((batch, embed), BF16), pltpu.VMEM((half, embed), BF16),
                 pltpu.VMEM((embed, dim), BF16), pltpu.VMEM((embed, dim), BF16),
                 pltpu.VMEM((side, half, cols), BF16), pltpu.VMEM((group * half, cols), BF16),
@@ -367,12 +390,22 @@
                 pltpu.VMEM((rows // O_STEPS * heads, seq), BF16), pltpu.VMEM((rows // O_STEPS * heads, dim), F32),
                 pltpu.VMEM((side * O_STEPS, heads, rows // O_STEPS, dim), BF16),
                 pltpu.VMEM((group, rows // 2, dim), BF16), pltpu.VMEM((group, rows // 2, dim), BF16),
-                dma((side,)), dma((4,)), dma((side,)), dma((O_STEPS,)), dma((O_STEPS,)),
+                dma((side,)), dma((5,)), dma((side,)), dma((O_STEPS,)), dma((O_STEPS,)),
                 dma, dma, dma, dma((group,)), dma, dma, dma((side, O_STEPS)), dma, dma,
             ],
             compiler_params=pltpu.CompilerParams(collective_id=0, has_side_effects=True, vmem_limit_bytes=VMEM_LIMIT),
             name="attention_step",
         )(hidden, w_query.T, w_key, w_value, w_out, k_cache, v_cache, lengths, freq)
+        whole = jax.ShapeDtypeStruct(k_cache.shape, k_cache.dtype)
+        y_turned, k_out, v_out = pl.pallas_call(
+            write_kernel,
+            out_shape=(jax.ShapeDtypeStruct(*y_shape), whole, whole),
+            in_specs=[vmem] * 3,
+            out_specs=(hbm, hbm, hbm),
+            scratch_shapes=[dma((2 * O_STEPS + 1,))],
+            compiler_params=pltpu.CompilerParams(vmem_limit_bytes=1 << 20),
+            name="write_results",
+        )(y_turned, k_new, v_new)
         return y_turned.T, k_out, v_out
 
     return jax.shard_map(

time: 41.8 us -> 38 us (0.909)
  local copies, waits for them, and re-layouts: 4.73 us -> 0 us
  Pallas kernels: 36.3 us -> 37.3 us
    unnamed x3 -> x0, local copies, waits for them, and re-layouts: 4.73 us -> none
    pallas_call x0 -> x1, Pallas kernels: none -> 3.43 us  [local_step(): pl.pallas_call(write_kernel, out_shape=(jax.ShapeDtypeStruct(*y_shape), w...]
    pallas_call x1, Pallas kernels: 36.3 us -> 33.8 us  [local_step(): pl.pallas_call(functools.partial(step_kernel, side), out_shape=(pltpu.VME...]
where the time goes in v3:
time: 38 us; the launch traced here: 37.9 us
  Pallas kernels  37.3 us (98%)
  between operations  0.64 us (2%)
    pallas_call x1, Pallas kernels, local_step(): pl.pallas_call(functools.partial(step_kernel, side), out_shape=(pltpu.VME...  33.8 us
    pallas_call x1, Pallas kernels, local_step(): pl.pallas_call(write_kernel, out_shape=(jax.ShapeDtypeStruct(*y_shape), w...  3.43 us

profile of v3, /device:TPU:97, one launch (start us, length us, event | category | flops | bytes accessed | tf_op | source)
XLA Modules:
  0.0 37.9 jit_solution(1164498697382622388)
XLA Ops:
  0.6 33.8 %attention_step.1 = (bf16[64,2048]{1,0:T(8,128)(2,1)S(1)}, bf16[64,256,128]{2,1,0:T(8,128)(2,1)S(1)}, bf16[64,256,128]{2,1,0:T(8,128)(2,1)S(1)}) custom-call(bf16[2048,2048]{1,0:T(8,128)(2,1)} %hidden.1, bf16[64,2048]{1,0:T(8,128)(2,1)} %bitcast.2, bf16[2048,128]{1,0:T(8,128)(2,1)} %w_key.1, bf16[2048,128]{1,0:T(8,128)(2,1)} %w_value.1, ...), custom_call_target="tpu_custom_call" | custom-call | tf_op jit(solution)/shard_map/attention_step/pallas_call | solution.py:377
  34.5 3.4 %write_results.1 = (bf16[64,2048]{1,0:T(8,128)(2,1)}, bf16[64,256,128]{2,1,0:T(8,128)(2,1)}, bf16[64,256,128]{2,1,0:T(8,128)(2,1)}) custom-call(bf16[64,2048]{1,0:T(8,128)(2,1)S(1)} %get-tuple-element.9.y_in, bf16[64,256,128]{2,1,0:T(8,128)(2,1)S(1)} %get-tuple-element.10.k_in, bf16[64,256,128]{2,1,0:T(8,128)(2,1)S(1)} %get-tuple-element.11.v_in), custom_call_target="tpu_custom_call" | custom-call | tf_op jit(solution)/shard_map/write_results/pallas_call | solution.py:400

commit v4 on v3

--- a/solution.py
+++ b/solution.py
@@ -14,13 +14,14 @@
 O_STEPS = 4
 SUB = 8
 VMEM_LIMIT = 55 << 20
+FIRST_W = 0
 
 
 def step_kernel(side, hidden, wq_turned, w_key, w_value, w_out, k_in, v_in, lengths, freq_in, y_out, k_buf, v_buf,
                 lens, freq, lens_f, h_buf, wq_buf, wk_buf, wv_buf, wo_buf, w_buf, k_new, v_new,
-                q_send, q_recv, q_rows, s_rows, p_rows, o_rows, o_buf, y_send, y_recv,
+                q_send, q_recv, q_rows, s_rows, p_rows, o_rows, o_buf, y_acc, y_send, y_recv,
                 h_sem, small_sem, wo_sem, k_sem, v_sem,
-                q_ssem, q_rsem, w_ssem, w_rsem, w_xsem, o_ssem, o_rsem, y_ssem, y_rsem):
+                q_ssem, q_rsem, w_ssem, w_rsem, w_xsem, o_ssem, o_rsem, near_ssem, far_ssem, near_rsem, far_rsem):
     rows, seq, dim = k_in.shape
     half = dim // 2
     pack = rows // 2
@@ -75,8 +76,11 @@
     for peer in peers:
         pl.semaphore_signal(barrier, inc=1, device_id={"tp": peer}, device_id_type=MESH)
 
+    def w_row(t):
+        return (lax.rem(t, 2) * heads + t // 2) * half
+
     def w_slot(t):
-        return w_buf.at[pl.ds(pl.multiple_of(t * half, half), half)]
+        return w_buf.at[pl.ds(pl.multiple_of(w_row(t), half), half)]
 
     left, right, other = index(x + side - 1, y, core), index(x + 1, y, core), chip * 2 + (1 - core)
     n_w = [0]
@@ -102,7 +106,7 @@
         for target in (right, left):
             send_w(wo_buf.at[y], me, target)
         give_w(wo_buf.at[y], me)
-        w_buf[pl.ds(pl.multiple_of(me * half, half), half)] = wo_buf[y]
+        w_buf[pl.ds(pl.multiple_of(w_row(me), half), half)] = wo_buf[y]
 
     with jax.named_scope("wait_wq"):
         small[0].wait()
@@ -129,13 +133,10 @@
             with jax.named_scope("barrier"):
                 pl.semaphore_wait(barrier, len(peers))
 
-        def send_q(j, carry, i=i, yy=yy):
+        for j in range(2 * side if i < side - 1 else 2 * side - 1):
             slot = lax.rem(own + 1 + j, 2 * side)
             remote(q_send.at[i * 2 * side + slot], q_recv.at[me], q_ssem, q_rsem, yy * 2 * side + slot).start()
-            return carry
-
-        lax.fori_loop(0, 2 * side if i < side - 1 else 2 * side - 1, send_q, 0)
-        if i == side - 2:
+        if i == FIRST_W:
             first_w()
     own_w()
     q_recv[me] = q_send[(side - 1) * 2 * side + own]
@@ -204,6 +205,10 @@
 
             lax.fori_loop(0, step_rows, patch, 0)
 
+    with jax.named_scope("column"):
+        for d in (1, 3, 2):
+            forward_column(d)
+
     with jax.named_scope("wait_q"):
         wait_recv(q_recv.at[pl.ds(0, group - 1)], q_rsem)
     with jax.named_scope("rope"):
@@ -239,6 +244,8 @@
         scores = lax.dot_general(q_row, k_buf[r], (((1,), (1,)), ((), ())), preferred_element_type=F32) * scale
         last = jnp.concatenate([lens_f[pl.ds(r, 1), :]] * (seq // dim), axis=1)
         s_rows[pl.ds(part * heads, heads), :] = jnp.where(slots <= last, scores, -1e30)
+
+    low_step = lax.broadcasted_iota(jnp.int32, (step_rows, dim), 1) < half
 
     def attend(k):
         for part in range(step_rows):
@@ -253,93 +260,104 @@
                 part = first + u
                 summed = jnp.dot(p_rows[pl.ds(part * heads, heads), :], v_buf[k * step_rows + part], preferred_element_type=F32)
                 o_rows[pl.ds(part * heads, heads), :] = summed / total[u * heads:(u + 1) * heads]
-        for i in range(heads):
-            o_buf[y * O_STEPS + k, i] = o_rows[pl.ds(i, step_rows, stride=heads), :].astype(BF16)
+        for i in range(heads // 2):
+            even, odd = (o_rows[pl.ds(2 * i + j, step_rows, stride=heads), :] for j in range(2))
+            o_buf[y * O_STEPS + k, i] = jnp.where(low_step, even, pltpu.roll(odd, half, 1)).astype(BF16)
+            o_buf[y * O_STEPS + k, heads // 2 + i] = jnp.where(low_step, pltpu.roll(even, half, 1), odd).astype(BF16)
         send_o(y, k, up)
         send_o(y, k, down)
 
     with jax.named_scope("attend0"):
         attend(0)
-    with jax.named_scope("column"):
-        for d in (1, 3, 2):
-            forward_column(d)
-    with jax.named_scope("attend1"):
-        attend(1)
     with jax.named_scope("relay0"):
         relay_right(0)
         pass_on(x + 1, 0)
+    with jax.named_scope("attend1"):
+        attend(1)
+    with jax.named_scope("relay1"):
+        relay_right(1)
     with jax.named_scope("attend2"):
         attend(2)
         attend(3)
-    with jax.named_scope("relay1"):
-        relay_right(1)
+    with jax.named_scope("relay2"):
         relay_left(3)
-    with jax.named_scope("relay2"):
-        relay_o(0)
         relay_left(2)
     with jax.named_scope("relay3"):
-        relay_o(1)
+        relay_o(0)
         pass_on(x + side - 1, 3)
         pass_on(x + side - 1, 2)
         pass_on(x + 1, 1)
     with jax.named_scope("relay4"):
+        relay_o(1)
         relay_o(2)
+    with jax.named_scope("relay5"):
         relay_o(3)
     with jax.named_scope("wait_w_far"):
         for d in (0, 1, 3, 2):
             pass_on(x + 2, d)
-    with jax.named_scope("wait_w_other"):
-        wait_recv(w_buf.at[pl.ds(0, heads * half)], w_xsem)
-
-    n_y = [0]
-
-    def project(*sources):
-        lhs = [jnp.concatenate([o_buf[pl.ds(yy * O_STEPS, O_STEPS), i].reshape(rows, dim) for i in range(heads)], axis=1)
-               for yy in sources]
-        res = jnp.dot(jnp.concatenate(lhs, axis=0), w_buf[...], preferred_element_type=F32)
-        for m, yy in enumerate(sources):
-            n = n_y[0]
-            n_y[0] += 1
-            row_owner = index(x, yy, core)
+    sources = [y, y_up, y_down, y_far]
+    near = side - 1
+    depth = heads * half
+
+    def partial(some, c):
+        lhs = [jnp.concatenate([o_buf[pl.ds(sources[n] * O_STEPS, O_STEPS), c * (heads // 2) + i].reshape(rows, dim)
+                                for i in range(heads // 2)], axis=1) for n in some]
+        return jnp.dot(jnp.concatenate(lhs, axis=0), w_buf[pl.ds(pl.multiple_of(c * depth, depth), depth), :],
+                       preferred_element_type=F32)
+
+    def place(some, res):
+        for m, n in enumerate(some):
             for slot in range(0, 2 * side, 2):
                 turned = res[m * rows:(m + 1) * rows, slot * half:(slot + 2) * half].T.astype(BF16)
                 for c in range(2):
                     part = turned[c * half:(c + 1) * half]
-                    y_send[n * 2 * side + slot + c] = jnp.concatenate([part[:half // 2], part[half // 2:]], axis=1)
-
-            def send_y(j, carry, n=n, row_owner=row_owner):
-                slot = lax.rem(own + 1 + j, 2 * side)
-                remote(y_send.at[n * 2 * side + slot], y_recv.at[row_owner], y_ssem, y_rsem, y * 2 * side + slot).start()
-                return carry
-
-            lax.fori_loop(0, 2 * side - 1, send_y, 0)
-            y_recv[row_owner] = y_send[n * 2 * side + own]
+                    y_send[slot + c, n] = jnp.concatenate([part[:half // 2], part[half // 2:]], axis=1)
 
     with jax.named_scope("wait_o_near"):
         wait_o(y_up, 0)
         wait_o(y_up, 2)
         wait_o(y_down, 1)
         wait_o(y_down, 3)
-    with jax.named_scope("project_near"):
-        project(y, y_up, y_down)
+    with jax.named_scope("near_own"):
+        y_acc[...] = partial(range(near), core)
+    with jax.named_scope("wait_w_other"):
+        wait_recv(w_buf.at[pl.ds(0, depth)], w_xsem)
+    with jax.named_scope("near_other"):
+        place(range(near), y_acc[...] + partial(range(near), 1 - core))
+        for j in range(1, 2 * side):
+            slot = lax.rem(own + j, 2 * side)
+            remote(y_send.at[slot, pl.ds(0, near)], y_recv.at[own, pl.ds(0, near)], near_ssem, near_rsem, y * 2 * side + slot).start()
     with jax.named_scope("wait_o_far"):
         for k in range(O_STEPS):
             wait_o(y_far, k)
     with jax.named_scope("project_far"):
-        project(y_far)
+        place([near], partial([near], core) + partial([near], 1 - core))
+        for j in range(1, 2 * side):
+            slot = lax.rem(own + j, 2 * side)
+            remote(y_send.at[slot, near], y_recv.at[own, near], far_ssem, far_rsem, y * 2 * side + slot).start()
+        y_recv[own] = y_send[own]
+
+    def finish(n):
+        for i in range(side):
+            a, b = y_recv[2 * i, n], y_recv[2 * i + 1, n]
+            span = pl.ds(pl.multiple_of((sources[n] * side + i) * 2 * rows, 2 * rows), 2 * rows)
+            y_out[pl.ds(0, half // 2), span] = jnp.concatenate([a[:, :rows], b[:, :rows]], axis=1)
+            y_out[pl.ds(half // 2, half // 2), span] = jnp.concatenate([a[:, rows:], b[:, rows:]], axis=1)
+
+    others = pl.ds(0, 2 * side - 1)
     with jax.named_scope("drain"):
         wait_send(q_send.at[pl.ds(0, group - 1)], q_ssem)
         wait_send(w_buf.at[pl.ds(0, n_w[0] * half)], w_ssem)
         wait_send(o_buf.at[pl.ds(0, 3 * O_STEPS)], o_ssem)
-    with jax.named_scope("wait_y"):
-        wait_recv(y_recv.at[pl.ds(0, side * (2 * side - 1))], y_rsem)
-    with jax.named_scope("finish"):
-        for i in range(heads):
-            a, b = y_recv[2 * i], y_recv[2 * i + 1]
-            two_rows = pl.ds(i * 2 * rows, 2 * rows)
-            y_out[pl.ds(0, half // 2), two_rows] = jnp.concatenate([a[:, :rows], b[:, :rows]], axis=1)
-            y_out[pl.ds(half // 2, half // 2), two_rows] = jnp.concatenate([a[:, rows:], b[:, rows:]], axis=1)
-        wait_send(y_send.at[pl.ds(0, side * (2 * side - 1))], y_ssem)
+        wait_send(y_send.at[others, pl.ds(0, near)], near_ssem)
+    with jax.named_scope("wait_y_near"):
+        wait_recv(y_recv.at[others, pl.ds(0, near)], near_rsem)
+    for n in range(near):
+        finish(n)
+    with jax.named_scope("wait_y_far"):
+        wait_recv(y_recv.at[others, near], far_rsem)
+    finish(near)
+    wait_send(y_send.at[others, near], far_ssem)
 
 
 def write_kernel(y_in, k_in, v_in, y_out, k_out, v_out, sems):
@@ -373,6 +391,7 @@
         freq = (10000.0 ** (-(np.arange(half) * 2.0) / dim)).astype(np.float32)
         freq = jnp.asarray(np.concatenate([freq, freq])[None, :])
         cache_shape = pltpu.VMEM(k_cache.shape, k_cache.dtype)
+        packed = pltpu.VMEM((2 * side, side, half // 2, dim), BF16)
         y_shape = ((w_out.shape[1] // group, batch), BF16)
         y_turned, k_new, v_new = pl.pallas_call(
             functools.partial(step_kernel, side),
@@ -389,9 +408,9 @@
                 pltpu.VMEM((rows * heads, dim), F32), pltpu.VMEM((rows // O_STEPS * heads, seq), F32),
                 pltpu.VMEM((rows // O_STEPS * heads, seq), BF16), pltpu.VMEM((rows // O_STEPS * heads, dim), F32),
                 pltpu.VMEM((side * O_STEPS, heads, rows // O_STEPS, dim), BF16),
-                pltpu.VMEM((group, rows // 2, dim), BF16), pltpu.VMEM((group, rows // 2, dim), BF16),
+                pltpu.VMEM(((side - 1) * rows, cols), F32), packed, packed,
                 dma((side,)), dma((5,)), dma((side,)), dma((O_STEPS,)), dma((O_STEPS,)),
-                dma, dma, dma, dma((group,)), dma, dma, dma((side, O_STEPS)), dma, dma,
+                dma, dma, dma, dma((group,)), dma, dma, dma((side, O_STEPS)), dma, dma, dma, dma,
             ],
             compiler_params=pltpu.CompilerParams(collective_id=0, has_side_effects=True, vmem_limit_bytes=VMEM_LIMIT),
             name="attention_step",

time: 38 us -> 37 us (0.974)
  Pallas kernels: 37.3 us -> 36.3 us
    pallas_call x1, Pallas kernels: 33.8 us -> 32.9 us  [local_step(): pl.pallas_call(functools.partial(step_kernel, side), out_shape=(pltpu.VME...]
where the time goes in v4:
time: 37 us; the launch traced here: 36.9 us
  Pallas kernels  36.3 us (98%)
  between operations  0.64 us (2%)
    pallas_call x1, Pallas kernels, local_step(): pl.pallas_call(functools.partial(step_kernel, side), out_shape=(pltpu.VME...  32.9 us
    pallas_call x1, Pallas kernels, local_step(): pl.pallas_call(write_kernel, out_shape=(jax.ShapeDtypeStruct(*y_shape), w...  3.43 us

profile of v4, /device:TPU:97, one launch (start us, length us, event | category | flops | bytes accessed | tf_op | source)
XLA Modules:
  0.0 36.9 jit_solution(10013662356299564979)
XLA Ops:
  0.6 32.9 %attention_step.1 = (bf16[64,2048]{1,0:T(8,128)(2,1)S(1)}, bf16[64,256,128]{2,1,0:T(8,128)(2,1)S(1)}, bf16[64,256,128]{2,1,0:T(8,128)(2,1)S(1)}) custom-call(bf16[2048,2048]{1,0:T(8,128)(2,1)} %hidden.1, bf16[64,2048]{1,0:T(8,128)(2,1)} %bitcast.2, bf16[2048,128]{1,0:T(8,128)(2,1)} %w_key.1, bf16[2048,128]{1,0:T(8,128)(2,1)} %w_value.1, ...), custom_call_target="tpu_custom_call" | custom-call | tf_op jit(solution)/shard_map/attention_step/pallas_call | solution.py:396
  33.5 3.4 %write_results.1 = (bf16[64,2048]{1,0:T(8,128)(2,1)}, bf16[64,256,128]{2,1,0:T(8,128)(2,1)}, bf16[64,256,128]{2,1,0:T(8,128)(2,1)}) custom-call(bf16[64,2048]{1,0:T(8,128)(2,1)S(1)} %get-tuple-element.9.y_in, bf16[64,256,128]{2,1,0:T(8,128)(2,1)S(1)} %get-tuple-element.10.k_in, bf16[64,256,128]{2,1,0:T(8,128)(2,1)S(1)} %get-tuple-element.11.v_in), custom_call_target="tpu_custom_call" | custom-call | tf_op jit(solution)/shard_map/write_results/pallas_call | solution.py:419

commit v5 on v4

--- a/solution.py
+++ b/solution.py
@@ -21,7 +21,7 @@
                 lens, freq, lens_f, h_buf, wq_buf, wk_buf, wv_buf, wo_buf, w_buf, k_new, v_new,
                 q_send, q_recv, q_rows, s_rows, p_rows, o_rows, o_buf, y_acc, y_send, y_recv,
                 h_sem, small_sem, wo_sem, k_sem, v_sem,
-                q_ssem, q_rsem, w_ssem, w_rsem, w_xsem, o_ssem, o_rsem, near_ssem, far_ssem, near_rsem, far_rsem):
+                q_ssem, q_rsem, q_rsem_late, w_ssem, w_rsem, w_xsem, o_ssem, o_rsem, near_ssem, far_ssem, near_rsem, far_rsem):
     rows, seq, dim = k_in.shape
     half = dim // 2
     pack = rows // 2
@@ -63,18 +63,16 @@
         part = pl.ds(k * step_rows, step_rows)
         kv_copies.append((pltpu.make_async_copy(k_in.at[part], k_buf.at[part], k_sem.at[k]),
                           pltpu.make_async_copy(v_in.at[part], v_buf.at[part], v_sem.at[k])))
+    order = (0, 2, 1, 3)
     small[0].start()
     h_copies[0].start()
-    for copy in wo_copies:
-        copy.start()
-    h_copies[1].start()
-    small[1].start()
-    small[4].start()
 
     barrier = pltpu.get_barrier_semaphore()
     peers = [(lax.rem(chip + i, heads)) * 2 + c for i in range(1, heads) for c in range(2)] + [chip * 2 + (1 - core)]
     for peer in peers:
         pl.semaphore_signal(barrier, inc=1, device_id={"tp": peer}, device_id_type=MESH)
+    for copy in wo_copies + [h_copies[1], small[1], small[4]]:
+        copy.start()
 
     def w_row(t):
         return (lax.rem(t, 2) * heads + t // 2) * half
@@ -112,6 +110,14 @@
         small[0].wait()
     wq = wq_buf[...].T
     own = x * 2 + core
+    quarter = pack // 2
+
+    def send_q(i, part, rsem):
+        some = pl.ds(part * quarter, quarter)
+        for j in range(2 * side if i < side - 1 else 2 * side - 1):
+            slot = lax.rem(own + 1 + j, 2 * side)
+            remote(q_send.at[i * 2 * side + slot, some], q_recv.at[me, some], q_ssem, rsem, ydest[i] * 2 * side + slot).start()
+
     for i, yy in enumerate(ydest):
         with jax.named_scope("wait_h"):
             h_copies[i].wait()
@@ -121,7 +127,7 @@
             for copy in small[2:4]:
                 copy.start()
         if i == 2:
-            for k in range(O_STEPS // 2):
+            for k in order[:2]:
                 for copy in kv_copies[k]:
                     copy.start()
         for part in range(2):
@@ -133,14 +139,14 @@
             with jax.named_scope("barrier"):
                 pl.semaphore_wait(barrier, len(peers))
 
-        for j in range(2 * side if i < side - 1 else 2 * side - 1):
-            slot = lax.rem(own + 1 + j, 2 * side)
-            remote(q_send.at[i * 2 * side + slot], q_recv.at[me], q_ssem, q_rsem, yy * 2 * side + slot).start()
+        send_q(i, 0, q_rsem)
         if i == FIRST_W:
             first_w()
     own_w()
+    for i in range(side):
+        send_q(i, 1, q_rsem_late)
     q_recv[me] = q_send[(side - 1) * 2 * side + own]
-    for k in range(O_STEPS // 2, O_STEPS):
+    for k in order[2:]:
         for copy in kv_copies[k]:
             copy.start()
 
@@ -191,52 +197,59 @@
         k_new[...] = jnp.where(low, key * cos - turned_key * sin, key * cos + turned_key * sin)
         v_new[...] = jnp.dot(h_own, wv_buf[...], preferred_element_type=F32)
     slot_rows = lax.broadcasted_iota(jnp.int32, (seq, dim), 0).astype(F32).astype(BF16)
+
+    def patch(k):
+        for copy in kv_copies[k]:
+            copy.wait()
+
+        def patch_row(j, carry):
+            r = k * step_rows + j
+            here = slot_rows == lens_f[pl.ds(r, 1), :].astype(BF16)
+            k_buf[r] = jnp.where(here, k_new[pl.ds(r, 1), :].astype(BF16), k_buf[r])
+            v_buf[r] = jnp.where(here, v_new[pl.ds(r, 1), :].astype(BF16), v_buf[r])
+            return carry
+
+        lax.fori_loop(0, step_rows, patch_row, 0)
+
     with jax.named_scope("patch"):
-        for k in range(O_STEPS):
-            for copy in kv_copies[k]:
-                copy.wait()
-
-            def patch(j, carry, k=k):
-                r = k * step_rows + j
-                here = slot_rows == lens_f[pl.ds(r, 1), :].astype(BF16)
-                k_buf[r] = jnp.where(here, k_new[pl.ds(r, 1), :].astype(BF16), k_buf[r])
-                v_buf[r] = jnp.where(here, v_new[pl.ds(r, 1), :].astype(BF16), v_buf[r])
-                return carry
-
-            lax.fori_loop(0, step_rows, patch, 0)
-
+        for k in order:
+            patch(k)
     with jax.named_scope("column"):
         for d in (1, 3, 2):
             forward_column(d)
 
-    with jax.named_scope("wait_q"):
-        wait_recv(q_recv.at[pl.ds(0, group - 1)], q_rsem)
-    with jax.named_scope("rope"):
+    def wait_q(part, rsem):
+        wait_recv(q_recv.at[pl.ds(0, group - 1), pl.ds(part * quarter, quarter)], rsem)
+
+    low_quarter = lax.broadcasted_iota(jnp.int32, (quarter, dim), 1) < half
+
+    def rope(part):
+        span = pl.ds(part * quarter, quarter)
+        c_part, s_part = c_pack[part * quarter:(part + 1) * quarter], s_pack[part * quarter:(part + 1) * quarter]
         for i in range(heads):
-            p1, p2 = q_recv[2 * i].astype(F32), q_recv[2 * i + 1].astype(F32)
-            r1, r2 = p1 * c_pack - p2 * s_pack, p2 * c_pack + p1 * s_pack
-            q_rows[pl.ds(i, pack, stride=heads), :] = jnp.where(low_pack, r1, pltpu.roll(r2, half, 1))
-            q_rows[pl.ds(pack * heads + i, pack, stride=heads), :] = jnp.where(low_pack, pltpu.roll(r1, half, 1), r2)
+            p1, p2 = q_recv[2 * i, span, :].astype(F32), q_recv[2 * i + 1, span, :].astype(F32)
+            r1, r2 = p1 * c_part - p2 * s_part, p2 * c_part + p1 * s_part
+            at = part * quarter * heads + i
+            q_rows[pl.ds(at, quarter, stride=heads), :] = jnp.where(low_quarter, r1, pltpu.roll(r2, half, 1))
+            q_rows[pl.ds(pack * heads + at, quarter, stride=heads), :] = jnp.where(low_quarter, pltpu.roll(r1, half, 1), r2)
 
     scale = dim ** -0.5
     slots = lax.broadcasted_iota(jnp.int32, (heads, seq), 1).astype(F32)
     up, down = index(x, y + 1, core), index(x, y + side - 1, core)
     y_up, y_down, y_far = lax.rem(y + 1, side), lax.rem(y + side - 1, side), lax.rem(y + 2, side)
 
-    def send_o(yy, k, target):
-        piece = o_buf.at[yy * O_STEPS + k]
+    def send_o(yy, k, target, some=slice(None)):
+        piece = o_buf.at[yy * O_STEPS + k, some]
         remote(piece, piece, o_ssem, o_rsem.at[yy, k], target).start()
 
     def wait_o(yy, k):
         wait_recv(o_buf.at[yy * O_STEPS + k], o_rsem.at[yy, k])
 
     def relay_o(k):
-        if k % 2 == 0:
-            wait_o(y_down, k)
-            send_o(y_down, k, up)
-        else:
-            wait_o(y_up, k)
-            send_o(y_up, k, down)
+        wait_o(y_down, k)
+        send_o(y_down, k, up, pl.ds(0, heads // 2))
+        wait_o(y_up, k)
+        send_o(y_up, k, down, pl.ds(heads // 2, heads // 2))
 
     def score(k, part):
         r = k * step_rows + part
@@ -267,19 +280,24 @@
         send_o(y, k, up)
         send_o(y, k, down)
 
+    with jax.named_scope("wait_q"):
+        wait_q(0, q_rsem)
     with jax.named_scope("attend0"):
+        rope(0)
         attend(0)
     with jax.named_scope("relay0"):
         relay_right(0)
         pass_on(x + 1, 0)
     with jax.named_scope("attend1"):
+        attend(2)
+    with jax.named_scope("wait_q_late"):
+        wait_q(1, q_rsem_late)
+    with jax.named_scope("attend2"):
+        rope(1)
         attend(1)
-    with jax.named_scope("relay1"):
-        relay_right(1)
-    with jax.named_scope("attend2"):
-        attend(2)
         attend(3)
     with jax.named_scope("relay2"):
+        relay_right(1)
         relay_left(3)
         relay_left(2)
     with jax.named_scope("relay3"):
@@ -288,13 +306,13 @@
         pass_on(x + side - 1, 2)
         pass_on(x + 1, 1)
     with jax.named_scope("relay4"):
+        relay_o(2)
         relay_o(1)
-        relay_o(2)
-    with jax.named_scope("relay5"):
-        relay_o(3)
     with jax.named_scope("wait_w_far"):
         for d in (0, 1, 3, 2):
             pass_on(x + 2, d)
+    with jax.named_scope("relay5"):
+        relay_o(3)
     sources = [y, y_up, y_down, y_far]
     near = side - 1
     depth = heads * half
@@ -313,11 +331,6 @@
                     part = turned[c * half:(c + 1) * half]
                     y_send[slot + c, n] = jnp.concatenate([part[:half // 2], part[half // 2:]], axis=1)
 
-    with jax.named_scope("wait_o_near"):
-        wait_o(y_up, 0)
-        wait_o(y_up, 2)
-        wait_o(y_down, 1)
-        wait_o(y_down, 3)
     with jax.named_scope("near_own"):
         y_acc[...] = partial(range(near), core)
     with jax.named_scope("wait_w_other"):
@@ -410,7 +423,7 @@
                 pltpu.VMEM((side * O_STEPS, heads, rows // O_STEPS, dim), BF16),
                 pltpu.VMEM(((side - 1) * rows, cols), F32), packed, packed,
                 dma((side,)), dma((5,)), dma((side,)), dma((O_STEPS,)), dma((O_STEPS,)),
-                dma, dma, dma, dma((group,)), dma, dma, dma((side, O_STEPS)), dma, dma, dma, dma,
+                dma, dma, dma, dma, dma((group,)), dma, dma, dma((side, O_STEPS)), dma, dma, dma, dma,
             ],
             compiler_params=pltpu.CompilerParams(collective_id=0, has_side_effects=True, vmem_limit_bytes=VMEM_LIMIT),
             name="attention_step",

time: 37 us -> 37.4 us (1.011)
  Pallas kernels: 36.3 us -> 36.7 us
    pallas_call x1, Pallas kernels: 32.9 us -> 33.2 us  [local_step(): pl.pallas_call(functools.partial(step_kernel, side), out_shape=(pltpu.VME...]
where the time goes in v5:
time: 37.4 us; the launch traced here: 37.3 us
  Pallas kernels  36.7 us (98%)
  between operations  0.64 us (2%)
    pallas_call x1, Pallas kernels, local_step(): pl.pallas_call(functools.partial(step_kernel, side), out_shape=(pltpu.VME...  33.2 us
    pallas_call x1, Pallas kernels, local_step(): pl.pallas_call(write_kernel, out_shape=(jax.ShapeDtypeStruct(*y_shape), w...  3.43 us

profile of v5, /device:TPU:97, one launch (start us, length us, event | category | flops | bytes accessed | tf_op | source)
XLA Modules:
  0.0 37.3 jit_solution(11516296621618486678)
XLA Ops:
  0.6 33.2 %attention_step.1 = (bf16[64,2048]{1,0:T(8,128)(2,1)S(1)}, bf16[64,256,128]{2,1,0:T(8,128)(2,1)S(1)}, bf16[64,256,128]{2,1,0:T(8,128)(2,1)S(1)}) custom-call(bf16[2048,2048]{1,0:T(8,128)(2,1)} %hidden.1, bf16[64,2048]{1,0:T(8,128)(2,1)} %bitcast.2, bf16[2048,128]{1,0:T(8,128)(2,1)} %w_key.1, bf16[2048,128]{1,0:T(8,128)(2,1)} %w_value.1, ...), custom_call_target="tpu_custom_call" | custom-call | tf_op jit(solution)/shard_map/attention_step/pallas_call | solution.py:409
  33.9 3.4 %write_results.1 = (bf16[64,2048]{1,0:T(8,128)(2,1)}, bf16[64,256,128]{2,1,0:T(8,128)(2,1)}, bf16[64,256,128]{2,1,0:T(8,128)(2,1)}) custom-call(bf16[64,2048]{1,0:T(8,128)(2,1)S(1)} %get-tuple-element.9.y_in, bf16[64,256,128]{2,1,0:T(8,128)(2,1)S(1)} %get-tuple-element.10.k_in, bf16[64,256,128]{2,1,0:T(8,128)(2,1)S(1)} %get-tuple-element.11.v_in), custom_call_target="tpu_custom_call" | custom-call | tf_op jit(solution)/shard_map/write_results/pallas_call | solution.py:432

commit v6 on v5

--- a/solution.py
+++ b/solution.py
@@ -12,6 +12,7 @@
 F32, BF16 = jnp.float32, jnp.bfloat16
 MESH = pl.DeviceIdType.MESH
 O_STEPS = 4
+WRITES = 1
 SUB = 8
 VMEM_LIMIT = 55 << 20
 FIRST_W = 0
@@ -83,12 +84,14 @@
     left, right, other = index(x + side - 1, y, core), index(x + 1, y, core), chip * 2 + (1 - core)
     n_w = [0]
 
-    def send_w(src, t, target):
-        n_w[0] += 1
-        remote(src, w_slot(t), w_ssem, w_rsem.at[t], target).start()
+    def send_w(src, t, target, first=0, size=None):
+        size = half if size is None else size
+        some = pl.ds(first, size)
+        n_w[0] += size
+        remote(src.at[some], w_slot(t).at[some], w_ssem, w_rsem.at[t], target).start()
 
     def give_w(src, t):
-        n_w[0] += 1
+        n_w[0] += half
         remote(src, w_slot(t), w_ssem, w_xsem, other).start()
 
     def wait_w(t):
@@ -114,8 +117,8 @@
 
     def send_q(i, part, rsem):
         some = pl.ds(part * quarter, quarter)
-        for j in range(2 * side if i < side - 1 else 2 * side - 1):
-            slot = lax.rem(own + 1 + j, 2 * side)
+        slots = [lax.rem(x + d, side) * 2 + c for d in (2, 1, 3) for c in range(2)] + [x * 2 + 1 - core]
+        for slot in slots + ([own] if i < side - 1 else []):
             remote(q_send.at[i * 2 * side + slot, some], q_recv.at[me, some], q_ssem, rsem, ydest[i] * 2 * side + slot).start()
 
     for i, yy in enumerate(ydest):
@@ -153,7 +156,7 @@
     def forward_column(d):
         t = index(x, y + d, core)
         wait_w(t)
-        for target in (right, left):
+        for target in (left, right):
             send_w(w_slot(t), t, target)
         give_w(w_slot(t), t)
 
@@ -162,6 +165,13 @@
         wait_w(t)
         send_w(w_slot(t), t, right)
         give_w(w_slot(t), t)
+
+    def relay_both(d):
+        for xx, target, first in ((x + side - 1, right, 0), (x + 1, left, half // 2)):
+            t = index(xx, y + d, core)
+            wait_w(t)
+            send_w(w_slot(t), t, target, first, half // 2)
+            give_w(w_slot(t), t)
 
     def relay_left(d):
         t = index(x + 1, y + d, core)
@@ -299,23 +309,25 @@
     with jax.named_scope("relay2"):
         relay_right(1)
         relay_left(3)
-        relay_left(2)
+        relay_both(2)
     with jax.named_scope("relay3"):
         relay_o(0)
         pass_on(x + side - 1, 3)
-        pass_on(x + side - 1, 2)
         pass_on(x + 1, 1)
     with jax.named_scope("relay4"):
         relay_o(2)
         relay_o(1)
+    with jax.named_scope("relay5"):
+        relay_o(3)
     with jax.named_scope("wait_w_far"):
         for d in (0, 1, 3, 2):
             pass_on(x + 2, d)
-    with jax.named_scope("relay5"):
-        relay_o(3)
     sources = [y, y_up, y_down, y_far]
     near = side - 1
     depth = heads * half
+
+    def row_peers():
+        return [lax.rem(x + d, side) * 2 + c for d in (2, 1, 3) for c in range(2)] + [x * 2 + 1 - core]
 
     def partial(some, c):
         lhs = [jnp.concatenate([o_buf[pl.ds(sources[n] * O_STEPS, O_STEPS), c * (heads // 2) + i].reshape(rows, dim)
@@ -337,16 +349,14 @@
         wait_recv(w_buf.at[pl.ds(0, depth)], w_xsem)
     with jax.named_scope("near_other"):
         place(range(near), y_acc[...] + partial(range(near), 1 - core))
-        for j in range(1, 2 * side):
-            slot = lax.rem(own + j, 2 * side)
+        for slot in row_peers():
             remote(y_send.at[slot, pl.ds(0, near)], y_recv.at[own, pl.ds(0, near)], near_ssem, near_rsem, y * 2 * side + slot).start()
     with jax.named_scope("wait_o_far"):
         for k in range(O_STEPS):
             wait_o(y_far, k)
     with jax.named_scope("project_far"):
         place([near], partial([near], core) + partial([near], 1 - core))
-        for j in range(1, 2 * side):
-            slot = lax.rem(own + j, 2 * side)
+        for slot in row_peers():
             remote(y_send.at[slot, near], y_recv.at[own, near], far_ssem, far_rsem, y * 2 * side + slot).start()
         y_recv[own] = y_send[own]
 
@@ -360,7 +370,7 @@
     others = pl.ds(0, 2 * side - 1)
     with jax.named_scope("drain"):
         wait_send(q_send.at[pl.ds(0, group - 1)], q_ssem)
-        wait_send(w_buf.at[pl.ds(0, n_w[0] * half)], w_ssem)
+        wait_send(w_buf.at[pl.ds(0, n_w[0])], w_ssem)
         wait_send(o_buf.at[pl.ds(0, 3 * O_STEPS)], o_ssem)
         wait_send(y_send.at[others, pl.ds(0, near)], near_ssem)
     with jax.named_scope("wait_y_near"):
@@ -375,10 +385,10 @@
 
 def write_kernel(y_in, k_in, v_in, y_out, k_out, v_out, sems):
     rows = k_in.shape[0]
-    part_rows = rows // O_STEPS
+    part_rows = rows // WRITES
     copies = []
     for src, dst in ((k_in, k_out), (v_in, v_out)):
-        for j in range(O_STEPS):
+        for j in range(WRITES):
             part = pl.ds(j * part_rows, part_rows)
             copies.append(pltpu.make_async_copy(src.at[part], dst.at[part], sems.at[len(copies)]))
     copies.append(pltpu.make_async_copy(y_in, y_out, sems.at[len(copies)]))
@@ -434,7 +444,7 @@
             out_shape=(jax.ShapeDtypeStruct(*y_shape), whole, whole),
             in_specs=[vmem] * 3,
             out_specs=(hbm, hbm, hbm),
-            scratch_shapes=[dma((2 * O_STEPS + 1,))],
+            scratch_shapes=[dma((2 * WRITES + 1,))],
             compiler_params=pltpu.CompilerParams(vmem_limit_bytes=1 << 20),
             name="write_results",
         )(y_turned, k_new, v_new)

time: 37.4 us -> 36.6 us (0.979)
  Pallas kernels: 36.7 us -> 35.9 us
    pallas_call x1, Pallas kernels: 33.2 us -> 32.4 us  [local_step(): pl.pallas_call(functools.partial(step_kernel, side), out_shape=(pltpu.VME...]
where the time goes in v6:
time: 36.6 us; the launch traced here: 36.5 us
  Pallas kernels  35.9 us (98%)
  between operations  0.64 us (2%)
    pallas_call x1, Pallas kernels, local_step(): pl.pallas_call(functools.partial(step_kernel, side), out_shape=(pltpu.VME...  32.4 us
    pallas_call x1, Pallas kernels, local_step(): pl.pallas_call(write_kernel, out_shape=(jax.ShapeDtypeStruct(*y_shape), w...  3.42 us

profile of v6, /device:TPU:97, one launch (start us, length us, event | category | flops | bytes accessed | tf_op | source)
XLA Modules:
  0.0 36.5 jit_solution(12471779431159493445)
XLA Ops:
  0.6 32.4 %attention_step.1 = (bf16[64,2048]{1,0:T(8,128)(2,1)S(1)}, bf16[64,256,128]{2,1,0:T(8,128)(2,1)S(1)}, bf16[64,256,128]{2,1,0:T(8,128)(2,1)S(1)}) custom-call(bf16[2048,2048]{1,0:T(8,128)(2,1)} %hidden.1, bf16[64,2048]{1,0:T(8,128)(2,1)} %bitcast.2, bf16[2048,128]{1,0:T(8,128)(2,1)} %w_key.1, bf16[2048,128]{1,0:T(8,128)(2,1)} %w_value.1, ...), custom_call_target="tpu_custom_call" | custom-call | tf_op jit(solution)/shard_map/attention_step/pallas_call | solution.py:419
  33.1 3.4 %write_results.1 = (bf16[64,2048]{1,0:T(8,128)(2,1)}, bf16[64,256,128]{2,1,0:T(8,128)(2,1)}, bf16[64,256,128]{2,1,0:T(8,128)(2,1)}) custom-call(bf16[64,2048]{1,0:T(8,128)(2,1)S(1)} %get-tuple-element.9.y_in, bf16[64,256,128]{2,1,0:T(8,128)(2,1)S(1)} %get-tuple-element.10.k_in, bf16[64,256,128]{2,1,0:T(8,128)(2,1)S(1)} %get-tuple-element.11.v_in), custom_call_target="tpu_custom_call" | custom-call | tf_op jit(solution)/shard_map/write_results/pallas_call | solution.py:442

commit v7 on v6

--- a/solution.py
+++ b/solution.py
@@ -167,7 +167,7 @@
         give_w(w_slot(t), t)
 
     def relay_both(d):
-        for xx, target, first in ((x + side - 1, right, 0), (x + 1, left, half // 2)):
+        for xx, target, first in ((x + 1, left, 0), (x + side - 1, right, half // 2)):
             t = index(xx, y + d, core)
             wait_w(t)
             send_w(w_slot(t), t, target, first, half // 2)

time: 36.6 us -> 36.4 us (level)
  no operation moved by 1% of the time
where the time goes in v7:
time: 36.4 us; the launch traced here: 36.3 us
  Pallas kernels  35.7 us (98%)
  between operations  0.64 us (2%)
    pallas_call x1, Pallas kernels, local_step(): pl.pallas_call(functools.partial(step_kernel, side), out_shape=(pltpu.VME...  32.3 us
    pallas_call x1, Pallas kernels, local_step(): pl.pallas_call(write_kernel, out_shape=(jax.ShapeDtypeStruct(*y_shape), w...  3.42 us

profile of v7, /device:TPU:97, one launch (start us, length us, event | category | flops | bytes accessed | tf_op | source)
XLA Modules:
  0.0 36.3 jit_solution(10954071601264182789)
XLA Ops:
  0.6 32.3 %attention_step.1 = (bf16[64,2048]{1,0:T(8,128)(2,1)S(1)}, bf16[64,256,128]{2,1,0:T(8,128)(2,1)S(1)}, bf16[64,256,128]{2,1,0:T(8,128)(2,1)S(1)}) custom-call(bf16[2048,2048]{1,0:T(8,128)(2,1)} %hidden.1, bf16[64,2048]{1,0:T(8,128)(2,1)} %bitcast.2, bf16[2048,128]{1,0:T(8,128)(2,1)} %w_key.1, bf16[2048,128]{1,0:T(8,128)(2,1)} %w_value.1, ...), custom_call_target="tpu_custom_call" | custom-call | tf_op jit(solution)/shard_map/attention_step/pallas_call | solution.py:419
  32.9 3.4 %write_results.1 = (bf16[64,2048]{1,0:T(8,128)(2,1)}, bf16[64,256,128]{2,1,0:T(8,128)(2,1)}, bf16[64,256,128]{2,1,0:T(8,128)(2,1)}) custom-call(bf16[64,2048]{1,0:T(8,128)(2,1)S(1)} %get-tuple-element.9.y_in, bf16[64,256,128]{2,1,0:T(8,128)(2,1)S(1)} %get-tuple-element.10.k_in, bf16[64,256,128]{2,1,0:T(8,128)(2,1)S(1)} %get-tuple-element.11.v_in), custom_call_target="tpu_custom_call" | custom-call | tf_op jit(solution)/shard_map/write_results/pallas_call | solution.py:442
